TPU v7x, 128 devices: a whole 4x4x4 slice. The times are simulated.
128 devices in a mesh: dp: 1, tp: 16 (over z, y), sp: 8 (over x, core).
Axes of the slice: x: 4, y: 4, z: 4, core: 2. Of those that a mesh axis runs over, the one named last changes fastest.
Arguments:
- x_in: bfloat16 [32768, 4096], P(('dp', 'sp'))
- w_z: bfloat16 [4096, 8192], P(None, 'tp')
- w_x: bfloat16 [4096, 8192], P(None, 'tp')
- w_bc: bfloat16 [4096, 256], replicated
- w_dt: bfloat16 [4096, 128], P(None, 'tp')
- a_neg: float32 [128], P('tp')
- dt_bias: float32 [128], P('tp')
- d_skip: float32 [128], P('tp')
- w_out: bfloat16 [8192, 4096], P('tp')
Outputs:
- output: bfloat16 [32768, 4096], P(('dp', 'sp', 'tp'))
All inputs are finite; a program needn't handle non-finite values.
Results may differ from a plain program's by a relative error of at most 0.0114328.
Values are sent between devices in bfloat16 or wider.
A program may use at most 1 GiB of HBM per device.

v0:
```python
import jax
import jax.numpy as jnp
from jax import lax
from jax.sharding import PartitionSpec as P

PIECE_LEN = 64


def local_ssd(x_ssm, dt_step, log_a, b_mat, c_mat):
    tokens, heads, head_dim = x_ssm.shape
    n_state = b_mat.shape[1]
    n_pieces = tokens // PIECE_LEN
    x_pc = x_ssm.reshape(n_pieces, PIECE_LEN, heads, head_dim)
    dt_pc = dt_step.reshape(n_pieces, PIECE_LEN, heads)
    la_pc = log_a.reshape(n_pieces, PIECE_LEN, heads)
    b_pc = b_mat.reshape(n_pieces, PIECE_LEN, n_state)
    c_pc = c_mat.reshape(n_pieces, PIECE_LEN, n_state)
    cum_log = jnp.cumsum(la_pc, axis=1)
    positions = jnp.arange(PIECE_LEN)
    causal = (positions[:, None] >= positions[None, :])[None, :, :, None]
    decay = jnp.where(causal, jnp.exp(jnp.minimum(cum_log[:, :, None, :] - cum_log[:, None, :, :], 0.0)), 0.0)
    gram = jnp.einsum('ctn,csn->cts', c_pc, b_pc, preferred_element_type=jnp.float32)
    weights = gram[:, :, :, None] * decay * dt_pc[:, None, :, :]
    y_intra = jnp.einsum('ctsh,cshp->cthp', weights, x_pc, preferred_element_type=jnp.float32)
    piece_tail = cum_log[:, -1, :]
    to_end = jnp.exp(piece_tail[:, None, :] - cum_log) * dt_pc
    piece_states = jnp.einsum('csh,cshp,csn->chpn', to_end, x_pc, b_pc, preferred_element_type=jnp.float32)
    piece_ends = jnp.cumsum(piece_tail, axis=0)
    piece_starts = piece_ends - piece_tail
    piece_ids = jnp.arange(n_pieces)
    earlier = (piece_ids[:, None] > piece_ids[None, :])[:, :, None]
    pass_w = jnp.where(earlier, jnp.exp(jnp.minimum(piece_starts[:, None, :] - piece_ends[None, :, :], 0.0)), 0.0)
    piece_in = jnp.einsum('cjh,jhpn->chpn', pass_w, piece_states, preferred_element_type=jnp.float32)
    y_pass = jnp.einsum('chpn,ctn->cthp', piece_in, c_pc, preferred_element_type=jnp.float32) * jnp.exp(cum_log)[:, :, :, None]
    block_state = jnp.einsum('jh,jhpn->hpn', jnp.exp(piece_ends[-1][None, :] - piece_ends), piece_states, preferred_element_type=jnp.float32)
    from_start = cum_log + piece_starts[:, None, :]
    y_local = (y_intra + y_pass).reshape(tokens, heads, head_dim)
    return y_local, block_state, piece_ends[-1], from_start.reshape(tokens, heads)


def solution(mesh):
    n_model = mesh.shape['tp']

    def device_fn(x_blk, w_z, w_x, w_bc, w_dt, a_neg, dt_bias, d_skip, w_out):
        tokens = x_blk.shape[0]
        heads = a_neg.shape[0]
        inner = w_x.shape[1]
        head_dim = inner // heads
        n_state = w_bc.shape[1] // 2
        z_gate = jnp.dot(x_blk, w_z, preferred_element_type=jnp.float32).astype(jnp.bfloat16)
        x_proj = jnp.dot(x_blk, w_x, preferred_element_type=jnp.float32).astype(jnp.bfloat16)
        x_ssm = x_proj.astype(jnp.float32).reshape(tokens, heads, head_dim)
        bc_val = jnp.dot(x_blk, w_bc, preferred_element_type=jnp.float32).astype(jnp.bfloat16).astype(jnp.float32)
        b_mat = bc_val[:, :n_state]
        c_mat = bc_val[:, n_state:]
        c_flip = c_mat[::-1]
        dt_step = jax.nn.softplus(jnp.dot(x_blk, w_dt, preferred_element_type=jnp.float32) + dt_bias)
        log_a = dt_step * a_neg
        y_fwd, state_fwd, block_log, from_fwd = local_ssd(x_ssm, dt_step, log_a, b_mat, c_mat)
        y_flip, state_bwd, _, from_bwd = local_ssd(x_ssm[::-1], dt_step[::-1], log_a[::-1], b_mat[::-1], c_flip)
        all_states = lax.all_gather(jnp.stack([state_fwd, state_bwd]), 'sp')
        all_logs = lax.all_gather(block_log, 'sp')
        n_seq = all_logs.shape[0]
        dev_index = lax.axis_index('sp')
        dev_ids = jnp.arange(n_seq)[:, None]
        log_ends = jnp.cumsum(all_logs, axis=0)
        log_starts = log_ends - all_logs
        my_start = jnp.sum(jnp.where(dev_ids < dev_index, all_logs, 0.0), axis=0)
        my_end = my_start + block_log
        w_fwd = jnp.where(dev_ids < dev_index, jnp.exp(jnp.minimum(my_start[None, :] - log_ends, 0.0)), 0.0)
        w_bwd = jnp.where(dev_ids > dev_index, jnp.exp(jnp.minimum(log_starts - my_end[None, :], 0.0)), 0.0)
        h_fwd = jnp.einsum('jh,jhpn->hpn', w_fwd, all_states[:, 0], preferred_element_type=jnp.float32)
        h_bwd = jnp.einsum('jh,jhpn->hpn', w_bwd, all_states[:, 1], preferred_element_type=jnp.float32)
        y_fwd = y_fwd + jnp.exp(from_fwd)[:, :, None] * jnp.einsum('hpn,tn->thp', h_fwd, c_mat, preferred_element_type=jnp.float32)
        y_bwd = (y_flip + jnp.exp(from_bwd)[:, :, None] * jnp.einsum('hpn,tn->thp', h_bwd, c_flip, preferred_element_type=jnp.float32))[::-1]
        y_sum = y_fwd + y_bwd + 2.0 * d_skip[:, None] * x_ssm
        gated = (y_sum.reshape(tokens, inner) * jax.nn.silu(z_gate.astype(jnp.float32))).astype(jnp.bfloat16)
        partial_out = jnp.dot(gated, w_out, preferred_element_type=jnp.float32)
        summed = lax.psum_scatter(partial_out, 'tp', scatter_dimension=0, tiled=True)
        rows = tokens // n_model
        resid = lax.dynamic_slice_in_dim(x_blk, lax.axis_index('tp') * rows, rows, axis=0)
        return (resid.astype(jnp.float32) + summed).astype(jnp.bfloat16)

    in_specs = (P(('dp', 'sp'), None), P(None, 'tp'), P(None, 'tp'), P(None, None), P(None, 'tp'), P('tp'), P('tp'), P('tp'), P('tp', None))
    out_specs = P(('dp', 'sp', 'tp'), None)
    return jax.shard_map(device_fn, mesh=mesh, in_specs=in_specs, out_specs=out_specs, check_vma=False)
```

profile of v0, /device:TPU:32, one launch (start us, length us, event | category | flops | bytes accessed | tf_op | source)
XLA Modules:
  0.0 905.4 jit_solution(14406298619152832324)
XLA Ops:
  6.5 15.2 %broadcast_multiply_fusion = (f32[4096,8]{0,1:T(8,128)S(1)}, f32[4096,8]{0,1:T(8,128)S(1)}) fusion(f32[8]{0:T(128)} %param.14, f32[8]{0:T(128)} %param.15, bf16[4096,4096]{1,0:T(8,128)(2,1)} %param.9, bf16[4096,8]{0,1:T(8,128)(2,1)} %param.13), kind=kOutput, calls=%fused_computation.83 | convolution fusion | flops 268697600 | bytes 33882176 | tf_op jit(solution)/shard_map/dot_general | solution.py:57
  46.0 10.8 %all-gather.1 = f32[8,1,8]{2,1,0:T(1,128)S(1)} all-gather(f32[1,1,8]{2,1,0:T(1,128)S(1)} %slice_bitcast_fusion.6), channel_id=1, replica_groups=mesh['dp'=1,'tp'=16,'sp'=8] {'sp'}, dimensions={0}, use_global_device_ids=true | all-gather | bytes 288 | tf_op jit(solution)/shard_map/all_gather | solution.py:62
  57.5 5.5 add_exponential_fusion
  66.3 5.5 add_exponential_fusion.1
  75.2 15.3 %convolution_convert_fusion.2 = bf16[4096,256]{1,0:T(8,128)(2,1)S(1)} fusion(bf16[4096,4096]{1,0:T(8,128)(2,1)} %param.9, bf16[4096,256]{1,0:T(8,128)(2,1)S(1)} %copy-done), kind=kOutput, calls=%fused_computation.64 | convolution fusion | flops 8590983168 | bytes 37748736 | tf_op jit(solution)/shard_map/dot_general | solution.py:53
  92.8 24.1 %convolution_convert_fusion.1 = bf16[4096,512]{0,1:T(8,128)(2,1)} fusion(bf16[4096,4096]{1,0:T(8,128)(2,1)} %param.9, bf16[4096,512]{1,0:T(8,128)(2,1)} %param.11), kind=kOutput, calls=%fused_computation.63 | convolution fusion | flops 17181966336 | bytes 41943040 | tf_op jit(solution)/shard_map/dot_general | solution.py:51
  116.9 12.6 %reshape_reshape.3 = bf16[64,64,8,64]{1,0,3,2:T(8,128)(2,1)} reshape(bf16[4096,512]{0,1:T(8,128)(2,1)} %convolution_convert_fusion.1) | data formatting | bytes 8388608 | tf_op jit(solution)/shard_map/reshape;reshape | solution.py:13
  129.5 19.9 %rev.20 = f32[4096,8,64]{0,2,1:T(8,128)} reverse(bf16[4096,8,64]{0,2,1:T(8,128)(2,1)} %bitcast.165), dimensions={0} | reverse | bytes 12582912 | tf_op jit(solution)/shard_map/rev | solution.py:60
  149.4 22.7 %reshape.138 = f32[64,64,8,64]{1,0,3,2:T(8,128)} reshape(f32[4096,8,64]{0,2,1:T(8,128)} %rev.20) | data formatting | bytes 16777216 | tf_op jit(solution)/shard_map/reshape | solution.py:13
  172.0 15.2 %fusion.13 = bf16[64,8,64,128]{3,2,1,0:T(8,128)(2,1)} fusion(bf16[64,64,128,1]{2,1,3,0:T(8,128)(2,1)S(1)} %bitcast.173, f32[64,64,8]{1,2,0:T(8,128)} %copy.63, bf16[64,64,8,64]{1,0,3,2:T(8,128)(2,1)} %reshape_reshape.3), kind=kOutput, calls=%fused_computation.15 | convolution fusion | flops 541065216 | bytes 13762560 | tf_op jit(solution)/shard_map/csh,cshp,csn->chpn/dot_general | solution.py:27
  187.3 8.2 fusion.29
  195.5 16.9 %fusion.11 = bf16[64,8,64,128]{3,2,1,0:T(8,128)(2,1)S(1)} fusion(bf16[64,64,128,1]{2,1,3,0:T(8,128)(2,1)S(1)} %bitcast.171, f32[64,64,8,64]{1,0,3,2:T(8,128)} %reshape.138, f32[64,64,8]{1,2,0:T(8,128)S(1)} %copy-done.14), kind=kOutput, calls=%fused_computation.13 | convolution fusion | flops 538968064 | bytes 17956864 | tf_op jit(solution)/shard_map/csh,cshp,csn->chpn/dot_general | solution.py:27
  215.6 4.6 fusion.23
  226.2 3.5 copy.58
  251.4 13.5 %fusion.37 = bf16[64,8,64,128]{3,0,2,1:T(8,128)(2,1)} fusion(bf16[64,64,8,1]{1,0,3,2:T(8,128)(2,1)S(1)} %copy-done.18, bf16[64,8,64,128]{3,2,1,0:T(8,128)(2,1)} %fusion.13), kind=kOutput, calls=%fused_computation.37 | convolution fusion | flops 536870912 | bytes 16842752 | tf_op jit(solution)/shard_map/cjh,jhpn->chpn/dot_general | solution.py:33
  265.6 13.1 %fusion.16 = f32[64,8,64,64]{3,2,1,0:T(8,128)} fusion(f32[64,64,8]{1,2,0:T(8,128)} %copy.60, f32[64,64,8]{1,2,0:T(8,128)} %copy.58, f32[64,64,64]{2,1,0:T(8,128)S(1)} %fusion.79, pred[64,64]{1,0:T(8,128)(4,1)S(1)} %copy-done.21, bf16[64,64,8,64]{1,0,3,2:T(8,128)(2,1)} %reshape_reshape.3), kind=kOutput, calls=%fused_computation.18 | convolution fusion | flops 278921216 | bytes 13897728 | tf_op jit(solution)/shard_map/ctsh,cshp->cthp/dot_general | solution.py:24
  278.8 23.0 %bitcast_add_fusion.1 = f32[64,64,8,64]{1,3,2,0:T(8,128)} fusion(f32[64,8,64,64]{3,2,1,0:T(8,128)} %fusion.16, bf16[64,64,128,1]{2,1,3,0:T(8,128)(2,1)S(1)} %bitcast.170, bf16[64,8,64,128]{3,0,2,1:T(8,128)(2,1)} %fusion.37, f32[64,64,8]{1,2,0:T(8,128)S(1)} %copy-done.16), kind=kOutput, calls=%fused_computation.1 | convolution fusion | flops 541065216 | bytes 26345472 | tf_op jit(solution)/shard_map/chpn,ctn->cthp/dot_general | solution.py:34
  301.7 18.1 %copy.70 = f32[64,64,8,64]{1,0,3,2:T(8,128)} copy(f32[64,64,8,64]{1,3,2,0:T(8,128)} %bitcast_add_fusion.1) | data formatting | bytes 16777216 | tf_op jit(solution)/shard_map/add | solution.py:37
  319.8 14.8 %reshape.133 = f32[4096,8,64]{0,2,1:T(8,128)} reshape(f32[64,64,8,64]{1,0,3,2:T(8,128)} %copy.70) | data formatting | bytes 16777216 | tf_op jit(solution)/shard_map/reshape | solution.py:37
  334.6 13.5 %fusion.40 = bf16[64,8,64,128]{3,0,2,1:T(8,128)(2,1)} fusion(bf16[64,64,8,1]{1,0,3,2:T(8,128)(2,1)S(1)} %copy-done.17, bf16[64,8,64,128]{3,2,1,0:T(8,128)(2,1)} %copy-done.2), kind=kOutput, calls=%fused_computation.38 | convolution fusion | flops 536870912 | bytes 16842752 | tf_op jit(solution)/shard_map/cjh,jhpn->chpn/dot_general | solution.py:33
  348.8 16.2 %fusion.4 = f32[64,8,64,64]{3,2,1,0:T(8,128)} fusion(f32[64,64,8,64]{1,0,3,2:T(8,128)} %reshape.138, f32[64,64,8]{1,2,0:T(8,128)S(1)} %copy-done.20, f32[64,64,8]{1,2,0:T(8,128)S(1)} %copy-done.19, f32[64,64,64]{2,1,0:T(8,128)S(1)} %fusion.80, pred[64,64]{1,0:T(8,128)(4,1)S(1)} %copy-done.21), kind=kOutput, calls=%fused_computation.6 | convolution fusion | flops 278921216 | bytes 18092032 | tf_op jit(solution)/shard_map/ctsh,cshp->cthp/dot_general | solution.py:24
  365.0 23.0 %bitcast_add_fusion = f32[64,64,8,64]{1,3,2,0:T(8,128)} fusion(f32[64,8,64,64]{3,2,1,0:T(8,128)} %fusion.4, bf16[64,64,128,1]{2,1,3,0:T(8,128)(2,1)S(1)} %bitcast.168, bf16[64,8,64,128]{3,0,2,1:T(8,128)(2,1)} %fusion.40, f32[64,64,8]{1,2,0:T(8,128)S(1)} %copy-done.15), kind=kOutput, calls=%fused_computation | convolution fusion | flops 541065216 | bytes 26345472 | tf_op jit(solution)/shard_map/chpn,ctn->cthp/dot_general | solution.py:34
  388.0 17.9 %copy.85 = f32[64,64,8,64]{1,0,3,2:T(8,128)} copy(f32[64,64,8,64]{1,3,2,0:T(8,128)} %bitcast_add_fusion) | data formatting | bytes 16777216 | tf_op jit(solution)/shard_map/add | solution.py:37
  405.8 14.8 %reshape.141 = f32[4096,8,64]{0,2,1:T(8,128)} reshape(f32[64,64,8,64]{1,0,3,2:T(8,128)} %copy.85) | data formatting | bytes 16777216 | tf_op jit(solution)/shard_map/reshape | solution.py:37
  423.2 7.9 multiply_add_fusion.1
  431.1 20.9 %rev.23 = f32[4096,8,64]{0,2,1:T(8,128)} reverse(f32[4096,8,64]{0,2,1:T(8,128)} %multiply_add_fusion.1), dimensions={0} | reverse | bytes 16777216 | tf_op jit(solution)/shard_map/rev | solution.py:75
  452.7 11.6 %multiply_add_fusion = f32[4096,8,64]{0,2,1:T(8,128)} fusion(f32[4096,8,64]{0,2,1:T(8,128)} %rev.23, f32[4096,8,64]{0,2,1:T(8,128)} %reshape.133, f32[8,64,128]{2,1,0:T(8,128)S(1)} %bitcast.176, f32[8]{0:T(128)S(1)} %broadcast_multiply_fusion.1, f32[4096,8]{0,1:T(8,128)S(1)} %exp.78, bf16[4096,8,64]{0,2,1:T(8,128)(2,1)} %bitcast.166, ...), kind=kOutput, calls=%fused_computation.43 | convolution fusion | flops 549453824 | bytes 30802432 | tf_op jit(solution)/shard_map/hpn,tn->thp/dot_general | solution.py:74
  464.3 9.0 copy.87
  473.3 27.0 %fusion.127 = bf16[4096,512]{1,0:T(8,128)(2,1)} fusion(f32[4096,512]{1,0:T(8,128)} %copy.87, bf16[4096,512]{1,0:T(8,128)(2,1)} %param.10, bf16[4096,4096]{1,0:T(8,128)(2,1)} %param.9), kind=kOutput, calls=%bitcast_fusion.14.clone.1 | convolution fusion | flops 17196646400 | bytes 50331648 | tf_op jit(solution)/shard_map/dot_general | solution.py:50
  500.3 30.0 %fusion.81 = f32[4096,4096]{1,0:T(8,128)} fusion(bf16[512,4096]{1,0:T(8,128)(2,1)} %param.17, bf16[4096,512]{1,0:T(8,128)(2,1)} %fusion.127), kind=kOutput, calls=%fused_computation.113 | convolution fusion | flops 17179869184 | bytes 75497472 | tf_op jit(solution)/shard_map/dot_general | solution.py:78
  530.3 363.1 %reduce-scatter.2.cloned.1.call-done = f32[256,4096]{1,0:T(8,128)} async-done(((f32[4096,4096]{1,0:T(8,128)}), f32[256,4096]{1,0:T(8,128)}) %reduce-scatter.2.cloned.1.call-update) | async-done | bytes 4194320 | tf_op jit(solution)/shard_map/reduce_scatter | solution.py:79
  893.4 4.7 add_convert_fusion
  (109 shorter events, 69.3 us)
Async XLA Ops:
  6.5 68.6 %copy-start = (bf16[4096,256]{1,0:T(8,128)(2,1)S(1)}, bf16[4096,256]{1,0:T(8,128)(2,1)}, u32[]{:S(2)}) copy-start(bf16[4096,256]{1,0:T(8,128)(2,1)} %param.12) | copy-start | bytes 6291460
  6.5 414.1 %all-gather.4.cloned.1.call-start = ((), (), s32[]{:S(2)}) async-start(), calls=%async_computation.2 | async-start | bytes 2359296 | tf_op jit(solution)/shard_map/all_gather | solution.py:61
  31.2 1.3 copy-start.3
  37.2 1.4 copy-start.5
  40.1 16.7 %copy-start.22 = (pred[8]{0:T(512)(128)(4,1)}, pred[8]{0:T(512)(128)(4,1)S(1)}, u32[]{:S(2)}) copy-start(pred[8]{0:T(512)(128)(4,1)S(1)} %get-tuple-element.28) | copy-start | bytes 28
  40.2 26.1 %copy-start.13 = (f32[64,64,8]{1,0,2:T(8,128)}, f32[64,64,8]{1,0,2:T(8,128)S(1)}, u32[]{:S(2)}) copy-start(f32[64,64,8]{1,0,2:T(8,128)S(1)} %reshape.135) | copy-start | bytes 393220
  90.5 1.3 copy-start.11
  91.8 80.2 %copy-start.8 = (bf16[4096,128]{1,0:T(8,128)(2,1)}, bf16[4096,128]{1,0:T(8,128)(2,1)S(1)}, u32[]{:S(2)}) copy-start(bf16[4096,128]{1,0:T(8,128)(2,1)S(1)} %get-tuple-element.11) | copy-start | bytes 3145732
  92.8 102.7 %copy-start.6 = (bf16[4096,128]{1,0:T(8,128)(2,1)}, bf16[4096,128]{1,0:T(8,128)(2,1)S(1)}, u32[]{:S(2)}) copy-start(bf16[4096,128]{1,0:T(8,128)(2,1)S(1)} %rev.21) | copy-start | bytes 3145732
  187.3 8.2 copy-start.14
  212.4 3.2 copy-start.2
  215.6 8.7 copy-start.4
  221.0 672.4 %reduce-scatter.2.cloned.1.call-start = ((), (), s32[]{:S(2)}) async-start(), calls=%async_computation.1 | async-start | bytes 71303168 | tf_op jit(solution)/shard_map/reduce_scatter | solution.py:79
  226.2 16.0 %copy-start.10 = (f32[64,64,8]{2,0,1:T(8,128)S(1)}, f32[64,64,8]{2,0,1:T(8,128)}, u32[]{:S(2)}) copy-start(f32[64,64,8]{2,0,1:T(8,128)} %get-tuple-element.15) | copy-start | bytes 393220
  242.2 9.2 %copy-start.18 = (bf16[64,64,8,1]{1,0,3,2:T(8,128)(2,1)S(1)}, bf16[64,64,8,1]{1,0,3,2:T(8,128)(2,1)}, u32[]{:S(2)}) copy-start(bf16[64,64,8,1]{1,0,3,2:T(8,128)(2,1)} %copy.89) | copy-start | bytes 196612
  251.4 13.5 %copy-start.9 = (bf16[4096,128]{1,0:T(8,128)(2,1)S(1)}, bf16[4096,128]{1,0:T(8,128)(2,1)}, u32[]{:S(2)}) copy-start(bf16[4096,128]{1,0:T(8,128)(2,1)} %copy-done.8) | copy-start | bytes 3145732
  251.4 14.2 %copy-start.21 = (pred[64,64]{1,0:T(8,128)(4,1)S(1)}, pred[64,64]{1,0:T(8,128)(4,1)}, u32[]{:S(2)}) copy-start(pred[64,64]{1,0:T(8,128)(4,1)} %iota_compare_fusion.1) | copy-start | bytes 12292
  265.6 13.1 %copy-start.16 = (f32[64,64,8]{1,2,0:T(8,128)S(1)}, f32[64,64,8]{1,2,0:T(8,128)}, u32[]{:S(2)}) copy-start(f32[64,64,8]{1,2,0:T(8,128)} %copy.68) | copy-start | bytes 393220
  319.8 14.8 %copy-start.17 = (bf16[64,64,8,1]{1,0,3,2:T(8,128)(2,1)S(1)}, bf16[64,64,8,1]{1,0,3,2:T(8,128)(2,1)}, u32[]{:S(2)}) copy-start(bf16[64,64,8,1]{1,0,3,2:T(8,128)(2,1)} %copy.100) | copy-start | bytes 196612
  334.6 13.5 %copy-start.7 = (bf16[4096,128]{1,0:T(8,128)(2,1)S(1)}, bf16[4096,128]{1,0:T(8,128)(2,1)}, u32[]{:S(2)}) copy-start(bf16[4096,128]{1,0:T(8,128)(2,1)} %copy-done.6) | copy-start | bytes 3145732
  334.6 14.2 %copy-start.19 = (f32[64,64,8]{1,2,0:T(8,128)S(1)}, f32[64,64,8]{1,2,0:T(8,128)}, u32[]{:S(2)}) copy-start(f32[64,64,8]{1,2,0:T(8,128)} %copy.76) | copy-start | bytes 393220
  334.6 14.2 %copy-start.20 = (f32[64,64,8]{1,2,0:T(8,128)S(1)}, f32[64,64,8]{1,2,0:T(8,128)}, u32[]{:S(2)}) copy-start(f32[64,64,8]{1,2,0:T(8,128)} %copy.78) | copy-start | bytes 393220
  348.8 16.2 %copy-start.15 = (f32[64,64,8]{1,2,0:T(8,128)S(1)}, f32[64,64,8]{1,2,0:T(8,128)}, u32[]{:S(2)}) copy-start(f32[64,64,8]{1,2,0:T(8,128)} %copy.83) | copy-start | bytes 393220
  405.8 14.8 %copy-start.23 = (f32[8]{0:T(128)S(1)}, f32[8]{0:T(128)}, u32[]{:S(2)}) copy-start(f32[8]{0:T(128)} %param.16) | copy-start | bytes 100
  431.0 21.6 %copy-start.12 = (bf16[4096,256]{1,0:T(8,128)(2,1)S(1)}, bf16[4096,256]{1,0:T(8,128)(2,1)}, u32[]{:S(2)}) copy-start(bf16[4096,256]{1,0:T(8,128)(2,1)} %copy-done.11) | copy-start | bytes 6291460
  530.3 367.9 %copy-start.1 = (bf16[4096,256]{1,0:T(8,128)(2,1)S(1)}, bf16[4096,256]{1,0:T(8,128)(2,1)}, u32[]{:S(2)}) copy-start(bf16[4096,256]{1,0:T(8,128)(2,1)} %param.12) | copy-start | bytes 6291460
Sparse Core Ops, SparseCore 0:
  221.1 25.1 all-gather.3
  530.4 362.9 reduce-scatter.1
where the time goes:
time: 916 us; the launch traced here: 905 us
  waiting for transfers between devices  363 us (40%)
  matrix products  281 us (31%)
  local copies, waits for them, and re-layouts  210 us (23%)
  other arithmetic  26.1 us (3%)
  between operations  14.2 us (2%)
  blocking collectives  10.8 us (1%)
    reduce_scatter x1, waiting for transfers between devices, device_fn(): lax.psum_scatter(partial_out, 'tp', scatter_dimension=0, tiled=True)  363 us
    dot_general x2, matrix products, local_ssd(): jnp.einsum('chpn,ctn->cthp', piece_in, c_pc, preferred_element_type=jnp.f...  46 us
    add x2, local copies, waits for them, and re-layouts, local_ssd(): y_local = (y_intra + y_pass).reshape(tokens, heads, head_dim)  36 us
    dot_general x2, matrix products, local_ssd(): jnp.einsum('csh,cshp,csn->chpn', to_end, x_pc, b_pc, preferred_element_ty...  32.1 us
    dot_general x1, matrix products, device_fn(): partial_out = jnp.dot(gated, w_out, preferred_element_type=jnp.float32)  30 us
    reshape x2, local copies, waits for them, and re-layouts, local_ssd(): y_local = (y_intra + y_pass).reshape(tokens, heads, head_dim)  29.5 us
    dot_general x2, matrix products, local_ssd(): jnp.einsum('ctsh,cshp->cthp', weights, x_pc, preferred_element_type=jnp.f...  29.3 us
    dot_general x1, matrix products, device_fn(): jnp.dot(x_blk, w_z, preferred_element_type=jnp.float32).astype(jnp.bfloat16)  27 us
  transfers between devices with their start and end apart: 2, of which 1 were waited for; matrix products, arithmetic and copies ran while one was open for 22% of the time, Pallas kernels for 0%

commit v1 on v0

v1 whole, which is shorter than its diff:
```python
import functools

import jax
import jax.numpy as jnp
from jax import lax
from jax.experimental import pallas as pl
from jax.experimental.pallas import tpu as pltpu
from jax.sharding import PartitionSpec as P

CHUNK = 128
MSG_PAD = 16


def split3(v):
    hi = v.astype(jnp.bfloat16).astype(jnp.float32)
    rest = v - hi
    mid = rest.astype(jnp.bfloat16).astype(jnp.float32)
    return [hi, mid, rest - mid]


def spread_operand(quantities, width):
    rows = [part for q in quantities for part in split3(q)]
    have = sum(r.shape[0] for r in rows)
    rows.append(jnp.zeros((CHUNK - have, width), jnp.float32))
    return jnp.concatenate(rows, axis=0).T.astype(jnp.bfloat16)


def cumsum_lanes(v, lane):
    step = 1
    while step < v.shape[1]:
        v = v + jnp.where(lane >= step, pltpu.roll(v, step, 1), 0.0)
        step *= 2
    return v


def softplus(v):
    return jnp.maximum(v, 0.0) + jnp.log1p(jnp.exp(-jnp.abs(v)))


def scan_kernel(n_blk, n_seq, heads, head_dim, x_ref, wz_ref, wx_ref, wbc_ref, wdt_ref, bias_ref, aneg_ref, skip_ref, g_ref,
                z_s, u_s, bc_s, sf_s, sb_s, f_s, g_s, dt_s, ci_s, ce_s, le_s, lt_s, e_s, msg_s, rcv_s, send_sem, recv_sem):
    i = pl.program_id(0)
    me = lax.axis_index('sp')
    rows = x_ref.shape[0]
    inner = heads * head_dim
    per_blk = rows // CHUNK
    n_state = bc_s.shape[1] // 2
    f32, bf16 = jnp.float32, jnp.bfloat16
    lane = lax.broadcasted_iota(jnp.int32, (heads, CHUNK), 1)

    def peer_copy(s):
        dest = lax.rem(me + s, n_seq)
        side = jnp.where(me + s < n_seq, 0, 1)
        return pltpu.make_async_remote_copy(
            src_ref=msg_s.at[side], dst_ref=rcv_s.at[s - 1], send_sem=send_sem.at[s - 1], recv_sem=recv_sem.at[s - 1],
            device_id={'sp': dest}, device_id_type=pl.DeviceIdType.MESH)

    @pl.when(i == 0)
    def _():
        barrier = pltpu.get_barrier_semaphore()
        for s in range(1, n_seq):
            pl.semaphore_signal(barrier, inc=1, device_id={'sp': lax.rem(me + s, n_seq)}, device_id_type=pl.DeviceIdType.MESH)
        k = lax.broadcasted_iota(jnp.int32, e_s.shape, 0)
        j = lax.broadcasted_iota(jnp.int32, e_s.shape, 1)
        hit = (k // (3 * heads) == j // inner) & (k % heads == (j % inner) // head_dim)
        e_s[...] = jnp.where(hit, 1.0, 0.0).astype(bf16)
        f_s[...] = jnp.zeros_like(f_s)
        g_s[...] = jnp.zeros_like(g_s)
        lt_s[...] = jnp.zeros_like(lt_s)

    @pl.when(i < n_blk)
    def _():
        base = pl.multiple_of(i * rows, rows)
        xb = x_ref[...]
        raw = jnp.dot(xb, wdt_ref[...], preferred_element_type=f32)
        bc_s[pl.ds(base, rows), :] = jnp.dot(xb, wbc_ref[...], preferred_element_type=f32).astype(bf16)
        u_s[pl.ds(base, rows), :] = jnp.dot(xb, wx_ref[...], preferred_element_type=f32).astype(bf16)
        z_s[pl.ds(base, rows), :] = jnp.dot(xb, wz_ref[...], preferred_element_type=f32).astype(bf16)
        for c in range(per_blk):
            cc = i * per_blk + c
            at = pl.multiple_of(base + c * CHUNK, CHUNK)
            dt = softplus(raw[c * CHUNK:(c + 1) * CHUNK, :].T[:heads, :] + bias_ref[...])
            la = dt * aneg_ref[...]
            ci = cumsum_lanes(la, lane)
            ce = ci - la
            end = jnp.broadcast_to(ci[:, CHUNK - 1:], ci.shape)
            dt_s[cc] = dt
            ci_s[cc] = ci
            ce_s[cc] = ce
            q = spread_operand([jnp.exp(end - ci) * dt, jnp.exp(ce) * dt, end], CHUNK)
            w = jnp.dot(q, e_s[:, :2 * inner], preferred_element_type=f32)
            le = jnp.dot(q[:16], e_s[:, 2 * inner:], preferred_element_type=f32)[:8]
            le_s[cc] = le
            u = u_s[pl.ds(at, CHUNK), :].astype(f32)
            b = bc_s[pl.ds(at, CHUNK), :n_state]
            dims = (((0,), (0,)), ((), ()))
            sf = lax.dot_general(b, (u * w[:, :inner]).astype(bf16), dims, preferred_element_type=f32)
            sb = lax.dot_general(b, (u * w[:, inner:]).astype(bf16), dims, preferred_element_type=f32)
            sf_s[cc] = sf
            sb_s[cc] = sb
            lt = lt_s[...]
            f_s[...] = f_s[...] * jnp.exp(le[:1]) + sf
            g_s[...] = g_s[...] + jnp.exp(lt[:1]) * sb
            lt_s[...] = lt + le

    @pl.when(i == n_blk - 1)
    def _():
        lt = lt_s[:1]
        parts = split3(lt)
        row = lax.broadcasted_iota(jnp.int32, (MSG_PAD, inner), 0)
        tail = jnp.where(row == 0, parts[0], jnp.where(row == 1, parts[1], jnp.where(row == 2, parts[2], 0.0))).astype(bf16)
        for side, ref in ((0, f_s), (1, g_s)):
            msg_s[side, :n_state, :] = ref[...].astype(bf16)
            msg_s[side, n_state:, :] = tail
        pl.semaphore_wait(pltpu.get_barrier_semaphore(), n_seq - 1)
        for s in range(1, n_seq):
            peer_copy(s).start()

    @pl.when(i == n_blk)
    def _():
        for s in range(1, n_seq):
            peer_copy(s).wait()

        def log_of(s):
            t = rcv_s[s - 1, n_state:, :].astype(f32)
            return t[0:1] + t[1:2] + t[2:3]

        f_s[...] = jnp.zeros_like(f_s)
        g_s[...] = jnp.zeros_like(g_s)
        acc = jnp.zeros((1, inner), f32)
        for s in range(1, n_seq):
            wgt = jnp.where(s <= me, jnp.exp(acc), 0.0)
            f_s[...] += wgt * rcv_s[s - 1, :n_state, :].astype(f32)
            acc = acc + log_of(s)
        acc = jnp.zeros((1, inner), f32)
        for s in range(n_seq - 1, 0, -1):
            wgt = jnp.where(s > me, jnp.exp(acc), 0.0)
            g_s[...] += wgt * rcv_s[s - 1, :n_state, :].astype(f32)
            acc = acc + log_of(s)

        n_ch = n_blk * per_blk

        def back(t, _):
            c = n_ch - 1 - t
            mine = sb_s[c]
            g = g_s[...]
            sb_s[c] = g
            g_s[...] = g * jnp.exp(le_s[c][:1]) + mine
            return 0

        lax.fori_loop(0, n_ch, back, 0)

    @pl.when(i >= n_blk)
    def _():
        blk = i - n_blk
        base = pl.multiple_of(blk * rows, rows)
        trow = lax.broadcasted_iota(jnp.int32, (CHUNK, CHUNK), 0)
        tcol = lax.broadcasted_iota(jnp.int32, (CHUNK, CHUNK), 1)
        later = trow > tcol
        left = tcol < head_dim
        twice = jnp.where(trow == tcol, 2.0, 1.0)
        for c in range(per_blk):
            cc = blk * per_blk + c
            at = pl.multiple_of(base + c * CHUNK, CHUNK)
            dt, ci, ce = dt_s[cc], ci_s[cc], ce_s[cc]
            end = jnp.broadcast_to(ci[:, CHUNK - 1:], ci.shape)
            q = spread_operand([dt, jnp.exp(ci), jnp.exp(end - ce)], CHUNK)
            w = jnp.dot(q, e_s[...], preferred_element_type=f32)
            col = jnp.concatenate([ci, ce, jnp.zeros((CHUNK - 2 * heads, CHUNK), f32)], axis=0).T
            u = u_s[pl.ds(at, CHUNK), :].astype(f32)
            udt = (u * w[:, :inner]).astype(bf16)
            b = bc_s[pl.ds(at, CHUNK), :n_state]
            cm = bc_s[pl.ds(at, CHUNK), n_state:]
            gram = lax.dot_general(cm, b, (((1,), (1,)), ((), ())), preferred_element_type=f32) * twice
            f_in = f_s[...]
            y = jnp.dot(cm, f_in.astype(bf16), preferred_element_type=f32) * w[:, inner:2 * inner]
            y = y + jnp.dot(cm, sb_s[cc].astype(bf16), preferred_element_type=f32) * w[:, 2 * inner:]
            y = y + skip_ref[...] * u
            f_s[...] = f_in * jnp.exp(le_s[cc][:1]) + sf_s[cc]
            outs = []
            for p in range(heads // 2):
                mats = []
                for h in (2 * p, 2 * p + 1):
                    d = jnp.where(later, col[:, h:h + 1] - ci[h:h + 1, :], ce[h:h + 1, :] - col[:, heads + h:heads + h + 1])
                    mats.append((gram * jnp.exp(jnp.minimum(d, 0.0))).astype(bf16))
                up = udt[:, p * CHUNK:(p + 1) * CHUNK]
                zero = jnp.zeros_like(up)
                rhs = jnp.concatenate([jnp.where(left, up, zero), jnp.where(left, zero, up)], axis=0)
                outs.append(jnp.dot(jnp.concatenate(mats, axis=1), rhs, preferred_element_type=f32))
            y = y + jnp.concatenate(outs, axis=1)
            z = z_s[pl.ds(at, CHUNK), :].astype(f32)
            g_ref[c * CHUNK:(c + 1) * CHUNK, :] = (y * (z / (1.0 + jnp.exp(-z)))).astype(bf16)


def scan_call(x_blk, w_z, w_x, w_bc, w_dt, a_neg, dt_bias, d_skip, n_seq):
    tokens, d_model = x_blk.shape
    heads = a_neg.shape[0]
    inner = w_x.shape[1]
    head_dim = inner // heads
    n_state = w_bc.shape[1] // 2
    rows = min(512, tokens)
    n_blk = tokens // rows
    n_ch = tokens // CHUNK
    w_dt = jnp.pad(w_dt, ((0, 0), (0, CHUNK - heads)))
    bias = jnp.broadcast_to(dt_bias[:, None], (heads, CHUNK))
    aneg = jnp.broadcast_to(a_neg[:, None], (heads, CHUNK))
    skip = jnp.repeat(2.0 * d_skip, head_dim)[None, :]
    f32, bf16 = jnp.float32, jnp.bfloat16

    def whole(a):
        return pl.BlockSpec(a.shape, lambda i: (0, 0), pipeline_mode=pl.Buffered(1))

    return pl.pallas_call(
        functools.partial(scan_kernel, n_blk, n_seq, heads, head_dim),
        grid=(2 * n_blk,),
        out_shape=jax.ShapeDtypeStruct((tokens, inner), bf16),
        in_specs=[pl.BlockSpec((rows, d_model), lambda i: (jnp.minimum(i, n_blk - 1), 0))]
        + [whole(a) for a in (w_z, w_x, w_bc, w_dt, bias, aneg, skip)],
        out_specs=pl.BlockSpec((rows, inner), lambda i: (jnp.maximum(i - n_blk, 0), 0)),
        scratch_shapes=[
            pltpu.VMEM((tokens, inner), bf16),
            pltpu.VMEM((tokens, inner), bf16),
            pltpu.VMEM((tokens, 2 * n_state), bf16),
            pltpu.VMEM((n_ch, n_state, inner), f32),
            pltpu.VMEM((n_ch, n_state, inner), f32),
            pltpu.VMEM((n_state, inner), f32),
            pltpu.VMEM((n_state, inner), f32),
            pltpu.VMEM((n_ch, heads, CHUNK), f32),
            pltpu.VMEM((n_ch, heads, CHUNK), f32),
            pltpu.VMEM((n_ch, heads, CHUNK), f32),
            pltpu.VMEM((n_ch, 8, inner), f32),
            pltpu.VMEM((8, inner), f32),
            pltpu.VMEM((CHUNK, 3 * inner), bf16),
            pltpu.VMEM((2, n_state + MSG_PAD, inner), bf16),
            pltpu.VMEM((n_seq - 1, n_state + MSG_PAD, inner), bf16),
            pltpu.SemaphoreType.DMA((n_seq - 1,)),
            pltpu.SemaphoreType.DMA((n_seq - 1,)),
        ],
        compiler_params=pltpu.CompilerParams(collective_id=0, has_side_effects=True, vmem_limit_bytes=60 * 1024 * 1024,
                                             dimension_semantics=('arbitrary',)),
        cost_estimate=pl.CostEstimate(flops=2 * tokens * d_model * (2 * inner + 3 * n_state) * 3, bytes_accessed=60 << 20, transcendentals=0),
    )(x_blk, w_z, w_x, w_bc, w_dt, bias, aneg, skip)


def solution(mesh):
    n_model = mesh.shape['tp']
    n_seq = mesh.shape['sp']

    def device_fn(x_blk, w_z, w_x, w_bc, w_dt, a_neg, dt_bias, d_skip, w_out):
        tokens = x_blk.shape[0]
        inner, d_model = w_out.shape
        rows = tokens // n_model
        half = d_model // 2
        core = lax.axis_index('sp') % 2
        pair = [(i, i ^ 1) for i in range(n_seq)]
        w_half = lax.dynamic_slice_in_dim(w_out, core * half, half, axis=1)
        w_all = lax.all_gather(w_half, 'tp', axis=0, tiled=True)
        g = scan_call(x_blk, w_z, w_x, w_bc, w_dt, a_neg, dt_bias, d_skip, n_seq)
        g_mine = lax.all_to_all(g.reshape(n_model, rows, inner), 'tp', 0, 0, tiled=True)
        g_mine = g_mine.transpose(1, 0, 2).reshape(rows, n_model * inner)
        g_other = lax.ppermute(g_mine, 'sp', pair)
        out_other = jnp.dot(g_other, w_all, preferred_element_type=jnp.float32)
        back = lax.ppermute(out_other, 'sp', pair)
        out_mine = jnp.dot(g_mine, w_all, preferred_element_type=jnp.float32)
        first = core == 0
        mixed = jnp.concatenate([jnp.where(first, out_mine, back), jnp.where(first, back, out_mine)], axis=1)
        resid = lax.dynamic_slice_in_dim(x_blk, lax.axis_index('tp') * rows, rows, axis=0)
        return (resid.astype(jnp.float32) + mixed).astype(jnp.bfloat16)

    in_specs = (P(('dp', 'sp'), None), P(None, 'tp'), P(None, 'tp'), P(None, None), P(None, 'tp'), P('tp'), P('tp'), P('tp'), P('tp', None))
    out_specs = P(('dp', 'sp', 'tp'), None)
    return jax.shard_map(device_fn, mesh=mesh, in_specs=in_specs, out_specs=out_specs, check_vma=False)
```

time: 916 us -> 301 us (0.33)
  waiting for transfers between devices: 363 us -> 19.9 us
  matrix products: 281 us -> 32.6 us
  local copies, waits for them, and re-layouts: 210 us -> 15.4 us
  Pallas kernels: 0 us -> 109 us
  blocking collectives: 10.8 us -> 102 us
  other arithmetic: 26.1 us -> 5.53 us
    reduce_scatter x1 -> x0, waiting for transfers between devices: 363 us -> none  [device_fn(): lax.psum_scatter(partial_out, 'tp', scatter_dimension=0, tiled=True)]
    dot_general x21 -> x2, matrix products: 281 us -> 32.6 us  [the longest x1 16.3 us: device_fn(): out_other = jnp.dot(g_other, w_all, preferred_element_type=jnp.float32)]
    pallas_call x0 -> x1, Pallas kernels: none -> 109 us  [scan_call(): pl.pallas_call(functools.partial(scan_kernel, n_blk, n_seq, heads, head_d...]
    all_to_all x0 -> x1, blocking collectives: none -> 102 us  [device_fn(): lax.all_to_all(g.reshape(n_model, rows, inner), 'tp', 0, 0, tiled=True)]
    reshape x11 -> x1, local copies, waits for them, and re-layouts: 71.8 us -> 6.44 us  [device_fn(): g.reshape(n_model, rows, inner)]
    rev x6 -> x0, local copies, waits for them, and re-layouts: 47.4 us -> none  [the longest x1 20.9 us: device_fn(): (y_flip + jnp.exp(from_bwd)[:, :, None] * jnp.einsum('hpn,tn->thp', h_bwd...]
    add x2 -> x0, local copies, waits for them, and re-layouts: 36 us -> none  [local_ssd(): y_local = (y_intra + y_pass).reshape(tokens, heads, head_dim)]
    another operation x3 -> x1, local copies, waits for them, and re-layouts: 17.9 us -> 0.67 us  [scan_call(): skip = jnp.repeat(2.0 * d_skip, head_dim)[None, :]]
  transfers between devices with their start and end apart: 2 -> 3, of which waited for: 1 -> 2; matrix products, arithmetic and copies ran while one was open for 22% -> 9% of each run, Pallas kernels for 0% -> 36%
where the time goes in v1:
time: 301 us; the launch traced here: 299 us
  Pallas kernels  109 us (36%)
  blocking collectives  102 us (34%)
  matrix products  32.6 us (11%)
  waiting for transfers between devices  19.9 us (7%)
  local copies, waits for them, and re-layouts  15.4 us (5%)
  between operations  13.5 us (4%)
  other arithmetic  5.53 us (2%)
    pallas_call x1, Pallas kernels, scan_call(): pl.pallas_call(functools.partial(scan_kernel, n_blk, n_seq, heads, head_d...  109 us
    all_to_all x1, blocking collectives, device_fn(): lax.all_to_all(g.reshape(n_model, rows, inner), 'tp', 0, 0, tiled=True)  102 us
    dot_general x1, matrix products, device_fn(): out_other = jnp.dot(g_other, w_all, preferred_element_type=jnp.float32)  16.3 us
    dot_general x1, matrix products, device_fn(): out_mine = jnp.dot(g_mine, w_all, preferred_element_type=jnp.float32)  16.3 us
    all_gather x1, waiting for transfers between devices, device_fn(): w_all = lax.all_gather(w_half, 'tp', axis=0, tiled=True)  13 us
    ppermute x1, waiting for transfers between devices, device_fn(): g_other = lax.ppermute(g_mine, 'sp', pair)  6.92 us
    reshape x1, local copies, waits for them, and re-layouts, device_fn(): g.reshape(n_model, rows, inner)  6.44 us
  transfers between devices with their start and end apart: 3, of which 2 were waited for; matrix products, arithmetic and copies ran while one was open for 9% of the time, Pallas kernels for 36%

profile of v1, /device:TPU:32, one launch (start us, length us, event | category | flops | bytes accessed | tf_op | source)
XLA Modules:
  0.0 298.9 jit_solution(4837587355324567188)
XLA Ops:
  6.5 0.0 copy-start.1
  6.5 0.0 copy-start.4
  6.5 0.0 all-gather.2.cloned.1.call-start
  6.5 0.0 copy-start.2
  6.5 0.0 copy-start.3
  6.5 3.2 %constant_dynamic-slice_fusion = bf16[512,2048]{1,0:T(8,128)(2,1)} fusion(bf16[512,4096]{1,0:T(8,128)(2,1)} %param.17, s32[]{:T(128)S(6)} %select_n.28), kind=kLoop, calls=%fused_computation.4 | loop fusion | bytes 4194308 | tf_op jit(solution)/shard_map/dynamic_slice | solution.py:256
  9.8 0.0 all-gather.2.cloned.1.call-update
  9.8 0.0 copy-done.1
  9.8 0.5 copy.11
  10.3 0.0 copy-done.4
  10.3 0.1 broadcast_in_dim.8
  10.4 0.7 broadcast_in_dim_reshape.3.skip_ref
  11.0 1.2 pad.4.wdt_ref
  12.2 0.0 copy-done.2
  12.2 0.7 broadcast_in_dim.6.bias_ref
  12.9 0.0 copy-done.3
  12.9 0.7 broadcast_in_dim.7.aneg_ref
  13.5 108.8 %shard_map.91 = bf16[4096,512]{1,0:T(8,128)(2,1)} custom-call(bf16[4096,4096]{1,0:T(8,128)(2,1)} %x_ref.1, bf16[4096,512]{1,0:T(8,128)(2,1)} %wz_ref.1, bf16[4096,512]{1,0:T(8,128)(2,1)} %wx_ref.1, bf16[4096,256]{1,0:T(8,128)(2,1)} %wbc_ref.1, bf16[4096,128]{1,0:T(8,128)(2,1)} %pad.4.wdt_ref, f32[8,128]{1,0:T(8,128)} %broadcast_in_dim.6.bias_ref, ...), custom_call_target="tpu_custom_call" | custom-call | flops 141733920768 | bytes 62914560 | tf_op jit(solution)/shard_map/pallas_call | solution.py:213
  122.3 6.4 %copy.12 = bf16[16,256,512]{1,2,0:T(8,128)(2,1)} copy(bf16[16,256,512]{2,1,0:T(8,128)(2,1)} %bitcast.10) | data formatting | bytes 8388608 | tf_op jit(solution)/shard_map/reshape | solution.py:259
  128.8 102.5 %all_to_all.5 = bf16[16,256,512]{1,2,0:T(8,128)(2,1)S(1)} all-to-all(bf16[16,256,512]{1,2,0:T(8,128)(2,1)} %copy.12), channel_id=1, replica_groups=mesh['dp'=1,'tp'=16,'sp'=8] {'tp'}, dimensions={0} | all-to-all | bytes 8388608 | tf_op jit(solution)/shard_map/all_to_all | solution.py:259
  231.2 0.0 copy-start
  231.2 2.1 copy-done
  233.3 0.6 collective-permute-start
  233.9 6.9 %collective-permute-done = bf16[256,8192]{0,1:T(8,128)(2,1)} collective-permute-done((bf16[256,8192]{0,1:T(8,128)(2,1)S(1)}, bf16[256,8192]{0,1:T(8,128)(2,1)}, u32[]{:S(2)}, u32[]{:S(2)}) %collective-permute-start) | collective-permute-done | bytes 4194336 | tf_op jit(solution)/shard_map/ppermute | solution.py:261
  240.9 13.0 %all-gather.2.cloned.1.call-done = bf16[8192,2048]{1,0:T(8,128)(2,1)} async-done(((bf16[512,2048]{1,0:T(8,128)(2,1)}), bf16[8192,2048]{1,0:T(8,128)(2,1)}) %all-gather.2.cloned.1.call-update) | async-done | bytes 33554448 | tf_op jit(solution)/shard_map/all_gather | solution.py:257
  253.8 16.3 %fusion.2 = f32[256,2048]{1,0:T(8,128)S(1)} fusion(bf16[256,8192]{0,1:T(8,128)(2,1)} %collective-permute-done, bf16[8192,2048]{1,0:T(8,128)(2,1)} %all-gather.2.cloned.1.call-done), kind=kOutput, calls=%fused_computation.7 | convolution fusion | flops 8589934592 | bytes 39845888 | tf_op jit(solution)/shard_map/dot_general | solution.py:262
  270.2 0.1 collective-permute-start.1
  270.3 16.3 %fusion.1 = f32[256,2048]{1,0:T(8,128)S(1)} fusion(bf16[256,8192]{0,1:T(8,128)(2,1)} %bitcast.9, bf16[8192,2048]{1,0:T(8,128)(2,1)} %all-gather.2.cloned.1.call-done), kind=kOutput, calls=%fused_computation.6 | convolution fusion | flops 8589934592 | bytes 39845888 | tf_op jit(solution)/shard_map/dot_general | solution.py:264
  286.6 0.0 collective-permute-done.1
  286.6 2.0 broadcast_select_fusion.1
  288.5 3.6 %fusion = bf16[256,4096]{1,0:T(8,128)(2,1)} fusion(f32[256,2048]{1,0:T(8,128)S(1)} %get-tuple-element.6, f32[256,2048]{1,0:T(8,128)S(1)} %get-tuple-element.5, bf16[4096,4096]{1,0:T(8,128)(2,1)} %x_ref.1, s32[]{:T(128)S(6)} %select_n.25), kind=kLoop, calls=%fused_computation.1 | loop fusion | flops 4194304 | bytes 8388612 | tf_op jit(solution)/shard_map/convert_element_type | solution.py:268
  (1 shorter events, 0.0 us)
Async XLA Ops:
  6.5 3.3 %copy-start.1 = (bf16[4096,8]{0,1:T(8,128)(2,1)S(1)}, bf16[4096,8]{0,1:T(8,128)(2,1)}, u32[]{:S(2)}) copy-start(bf16[4096,8]{0,1:T(8,128)(2,1)} %param.13) | copy-start | bytes 196612
  6.5 3.7 %copy-start.4 = (f32[8]{0:T(128)S(1)}, f32[8]{0:T(128)}, u32[]{:S(2)}) copy-start(f32[8]{0:T(128)} %param.16) | copy-start | bytes 100
  6.5 247.3 %all-gather.2.cloned.1.call-start = ((), (), s32[]{:S(2)}) async-start(), calls=%async_computation.1 | async-start | bytes 35651584 | tf_op jit(solution)/shard_map/all_gather | solution.py:257
  6.5 5.7 %copy-start.2 = (f32[8]{0:T(128)S(1)}, f32[8]{0:T(128)}, u32[]{:S(2)}) copy-start(f32[8]{0:T(128)} %param.15) | copy-start | bytes 100
  6.5 6.3 %copy-start.3 = (f32[8]{0:T(128)S(1)}, f32[8]{0:T(128)}, u32[]{:S(2)}) copy-start(f32[8]{0:T(128)} %param.14) | copy-start | bytes 100
  231.2 2.1 copy-start
  233.3 7.6 %collective-permute-start = (bf16[256,8192]{0,1:T(8,128)(2,1)S(1)}, bf16[256,8192]{0,1:T(8,128)(2,1)}, u32[]{:S(2)}, u32[]{:S(2)}) collective-permute-start(bf16[256,8192]{0,1:T(8,128)(2,1)S(1)} %bitcast.8), channel_id=1, source_target_pairs={{0,1},{1,0},{2,3},{3,2},{4,5},{5,4},{6,7},{7,6},{8,9},{9,8},{10,11... | collective-permute-start | bytes 12582920 | tf_op jit(solution)/shard_map/ppermute | solution.py:261
  270.2 16.4 %collective-permute-start.1 = (f32[256,2048]{1,0:T(8,128)S(1)}, f32[256,2048]{1,0:T(8,128)}, u32[]{:S(2)}, u32[]{:S(2)}) collective-permute-start(f32[256,2048]{1,0:T(8,128)S(1)} %fusion.2), channel_id=1, source_target_pairs={{0,1},{1,0},{2,3},{3,2},{4,5},{5,4},{6,7},{7,6},{8,9},{9,8},{10,11... | collective-permute-start | bytes 6291464 | tf_op jit(solution)/shard_map/ppermute | solution.py:263
Sparse Core Ops, SparseCore 0:
  9.9 243.8 all-gather.1

commit v2 on v1

--- a/solution.py
+++ b/solution.py
@@ -9,6 +9,7 @@
 
 CHUNK = 128
 MSG_PAD = 16
+RING = 4
 
 
 def split3(v):
@@ -37,8 +38,20 @@
     return jnp.maximum(v, 0.0) + jnp.log1p(jnp.exp(-jnp.abs(v)))
 
 
-def scan_kernel(n_blk, n_seq, heads, head_dim, x_ref, wz_ref, wx_ref, wbc_ref, wdt_ref, bias_ref, aneg_ref, skip_ref, g_ref,
-                z_s, u_s, bc_s, sf_s, sb_s, f_s, g_s, dt_s, ci_s, ce_s, le_s, lt_s, e_s, msg_s, rcv_s, send_sem, recv_sem):
+def tp_coords():
+    index = lax.axis_index('tp')
+    return index // RING, lax.rem(index, RING)
+
+
+def ring_peer(zy, axis, dist):
+    z, y = zy
+    if axis == 0:
+        return z * RING + lax.rem(y + dist, RING)
+    return lax.rem(z + dist, RING) * RING + y
+
+
+def scan_kernel(n_blk, n_seq, heads, head_dim, x_ref, wz_ref, wx_ref, wbc_ref, wdt_ref, bias_ref, aneg_ref, skip_ref, wo_ref, ga_ref, wg_ref,
+                z_s, u_s, bc_s, sf_s, sb_s, f_s, g_s, dt_s, ci_s, ce_s, le_s, lt_s, e_s, msg_s, rcv_s, send_sem, recv_sem, ws_sem, wr_sem, gs_sem, gr_sem, own_sem):
     i = pl.program_id(0)
     me = lax.axis_index('sp')
     rows = x_ref.shape[0]
@@ -55,11 +68,49 @@
             src_ref=msg_s.at[side], dst_ref=rcv_s.at[s - 1], send_sem=send_sem.at[s - 1], recv_sem=recv_sem.at[s - 1],
             device_id={'sp': dest}, device_id_type=pl.DeviceIdType.MESH)
 
+    zy = tp_coords()
+
+    def weight_copy(k):
+        part = wo_ref.shape[0] // 2
+        mine = pl.multiple_of(lax.rem(me, 2) * part, part)
+        if k < 8:
+            axis, back = k // 2 % 2, k % 2
+            dist = RING - 1 if back else 1
+            if k < 4:
+                rows_at, src, slot = pl.ds(mine, part), wo_ref, dist
+            else:
+                rows_at = pl.ds(pl.multiple_of(mine + back * (part // 2), part // 2), part // 2)
+                src, slot = wg_ref.at[axis * 3 + dist - 1], 2
+            dest = {'tp': ring_peer(zy, axis, dist)}
+        else:
+            axis, slot = ((k - 8) // 2, (1, 3)[k % 2]) if k < 12 else (k - 12, 2)
+            rows_at, src = pl.ds(mine, part), wg_ref.at[axis * 3 + slot - 1]
+            dest = {'sp': me + 1 - 2 * lax.rem(me, 2)}
+        return pltpu.make_async_remote_copy(
+            src_ref=src.at[rows_at, :], dst_ref=wg_ref.at[axis * 3 + slot - 1, rows_at, :], send_sem=ws_sem.at[k], recv_sem=wr_sem.at[k],
+            device_id=dest, device_id_type=pl.DeviceIdType.MESH)
+
+    def gate_copy(side, dist, group, at):
+        return pltpu.make_async_remote_copy(
+            src_ref=z_s.at[pl.ds(at, CHUNK), :], dst_ref=ga_ref.at[side, dist, pl.ds(pl.multiple_of(group * CHUNK, CHUNK), CHUNK), :],
+            send_sem=gs_sem.at[side, dist, group], recv_sem=gr_sem.at[side, dist, group],
+            device_id={'tp': ring_peer(zy, side, dist)}, device_id_type=pl.DeviceIdType.MESH)
+
+    def own_copy(side, group, at):
+        return pltpu.make_async_copy(z_s.at[pl.ds(at, CHUNK), :], ga_ref.at[side, 0, pl.ds(pl.multiple_of(group * CHUNK, CHUNK), CHUNK), :],
+                                     own_sem.at[side, group])
+
     @pl.when(i == 0)
     def _():
         barrier = pltpu.get_barrier_semaphore()
         for s in range(1, n_seq):
             pl.semaphore_signal(barrier, inc=1, device_id={'sp': lax.rem(me + s, n_seq)}, device_id_type=pl.DeviceIdType.MESH)
+        for axis in range(2):
+            for dist in range(1, RING):
+                pl.semaphore_signal(barrier, inc=1, device_id={'tp': ring_peer(zy, axis, dist)}, device_id_type=pl.DeviceIdType.MESH)
+        pl.semaphore_wait(barrier, n_seq - 1 + 2 * (RING - 1))
+        for k in range(4):
+            weight_copy(k).start()
         k = lax.broadcasted_iota(jnp.int32, e_s.shape, 0)
         j = lax.broadcasted_iota(jnp.int32, e_s.shape, 1)
         hit = (k // (3 * heads) == j // inner) & (k % heads == (j % inner) // head_dim)
@@ -112,12 +163,15 @@
         for side, ref in ((0, f_s), (1, g_s)):
             msg_s[side, :n_state, :] = ref[...].astype(bf16)
             msg_s[side, n_state:, :] = tail
-        pl.semaphore_wait(pltpu.get_barrier_semaphore(), n_seq - 1)
         for s in range(1, n_seq):
             peer_copy(s).start()
 
     @pl.when(i == n_blk)
     def _():
+        for k in range(4):
+            weight_copy(k).wait()
+        for k in range(4, 12):
+            weight_copy(k).start()
         for s in range(1, n_seq):
             peer_copy(s).wait()
 
@@ -189,10 +243,41 @@
                 outs.append(jnp.dot(jnp.concatenate(mats, axis=1), rhs, preferred_element_type=f32))
             y = y + jnp.concatenate(outs, axis=1)
             z = z_s[pl.ds(at, CHUNK), :].astype(f32)
-            g_ref[c * CHUNK:(c + 1) * CHUNK, :] = (y * (z / (1.0 + jnp.exp(-z)))).astype(bf16)
-
-
-def scan_call(x_blk, w_z, w_x, w_bc, w_dt, a_neg, dt_bias, d_skip, n_seq):
+            z_s[pl.ds(at, CHUNK), :] = (y * (z / (1.0 + jnp.exp(-z)))).astype(bf16)
+        for c in range(per_blk):
+            at = pl.multiple_of(base + c * CHUNK, CHUNK)
+            side = c % 2
+            owner = blk * (per_blk // 2) + c // 2
+            far = (lax.rem(owner // RING - zy[0] + RING, RING), lax.rem(lax.rem(owner, RING) - zy[1] + RING, RING))
+            dist, group = (far[1], far[0]) if side == 0 else (far[0], far[1])
+
+            @pl.when(dist == 0)
+            def _():
+                own_copy(side, group, at).start()
+
+            @pl.when(dist > 0)
+            def _():
+                gate_copy(side, dist, group, at).start()
+
+    @pl.when(i == n_blk + n_blk // 2)
+    def _():
+        for k in range(4, 8):
+            weight_copy(k).wait()
+        for k in range(12, 14):
+            weight_copy(k).start()
+
+    @pl.when(i == 2 * n_blk - 1)
+    def _():
+        for side in range(2):
+            for group in range(RING):
+                own_copy(side, group, 0).wait()
+                for dist in range(1, RING):
+                    gate_copy(side, dist, group, 0).wait()
+        for k in range(8, 14):
+            weight_copy(k).wait()
+
+
+def scan_call(x_blk, w_z, w_x, w_bc, w_dt, a_neg, dt_bias, d_skip, w_out, n_seq):
     tokens, d_model = x_blk.shape
     heads = a_neg.shape[0]
     inner = w_x.shape[1]
@@ -213,10 +298,11 @@
     return pl.pallas_call(
         functools.partial(scan_kernel, n_blk, n_seq, heads, head_dim),
         grid=(2 * n_blk,),
-        out_shape=jax.ShapeDtypeStruct((tokens, inner), bf16),
+        out_shape=(jax.ShapeDtypeStruct((2, RING, tokens // (2 * RING), inner), bf16),
+                   jax.ShapeDtypeStruct((2 * (RING - 1),) + w_out.shape, bf16)),
         in_specs=[pl.BlockSpec((rows, d_model), lambda i: (jnp.minimum(i, n_blk - 1), 0))]
-        + [whole(a) for a in (w_z, w_x, w_bc, w_dt, bias, aneg, skip)],
-        out_specs=pl.BlockSpec((rows, inner), lambda i: (jnp.maximum(i - n_blk, 0), 0)),
+        + [whole(a) for a in (w_z, w_x, w_bc, w_dt, bias, aneg, skip)] + [pl.BlockSpec(memory_space=pl.ANY)],
+        out_specs=(pl.BlockSpec(memory_space=pl.ANY), pl.BlockSpec(memory_space=pl.ANY)),
         scratch_shapes=[
             pltpu.VMEM((tokens, inner), bf16),
             pltpu.VMEM((tokens, inner), bf16),
@@ -235,37 +321,120 @@
             pltpu.VMEM((n_seq - 1, n_state + MSG_PAD, inner), bf16),
             pltpu.SemaphoreType.DMA((n_seq - 1,)),
             pltpu.SemaphoreType.DMA((n_seq - 1,)),
+            pltpu.SemaphoreType.DMA((14,)),
+            pltpu.SemaphoreType.DMA((14,)),
+            pltpu.SemaphoreType.DMA((2, RING, RING)),
+            pltpu.SemaphoreType.DMA((2, RING, RING)),
+            pltpu.SemaphoreType.DMA((2, RING)),
         ],
         compiler_params=pltpu.CompilerParams(collective_id=0, has_side_effects=True, vmem_limit_bytes=60 * 1024 * 1024,
                                              dimension_semantics=('arbitrary',)),
         cost_estimate=pl.CostEstimate(flops=2 * tokens * d_model * (2 * inner + 3 * n_state) * 3, bytes_accessed=60 << 20, transcendentals=0),
-    )(x_blk, w_z, w_x, w_bc, w_dt, bias, aneg, skip)
+    )(x_blk, w_z, w_x, w_bc, w_dt, bias, aneg, skip, w_out)
+
+
+def out_kernel(n_col, ga_ref, wo_ref, wg_ref, x_ref, out_ref, send_s, recv_s, own_s, x_s, x_sem, send_sem, recv_sem):
+    i = pl.program_id(0)
+    zy = tp_coords()
+    width = wo_ref.shape[1]
+    f32, bf16 = jnp.float32, jnp.bfloat16
+
+    def part_copy(side, dist, b):
+        return pltpu.make_async_remote_copy(
+            src_ref=send_s.at[side, dist - 1, b], dst_ref=recv_s.at[side, dist - 1, b],
+            send_sem=send_sem.at[side, dist - 1, b], recv_sem=recv_sem.at[side, dist - 1, b],
+            device_id={'tp': ring_peer(zy, 1 - side, dist)}, device_id_type=pl.DeviceIdType.MESH)
+
+    def x_copy():
+        rows = x_s.shape[0]
+        at = pl.multiple_of(lax.axis_index('tp') * rows, rows)
+        return pltpu.make_async_copy(x_ref.at[pl.ds(at, rows), :], x_s, x_sem)
+
+    @pl.when(i == 0)
+    def _():
+        x_copy().start()
+        barrier = pltpu.get_barrier_semaphore()
+        for axis in range(2):
+            for dist in range(1, RING):
+                pl.semaphore_signal(barrier, inc=1, device_id={'tp': ring_peer(zy, axis, dist)}, device_id_type=pl.DeviceIdType.MESH)
+
+    @pl.when(i < n_col)
+    def _():
+        for side in range(2):
+            acc = jnp.dot(ga_ref[side, 0], wo_ref[...], preferred_element_type=f32)
+            for dist in range(1, RING):
+                acc = acc + jnp.dot(ga_ref[side, dist], wg_ref[side * 3 + dist - 1], preferred_element_type=f32)
+            own_s[side, i] = acc[:CHUNK]
+            for dist in range(1, RING):
+                send_s[side, dist - 1, i] = acc[dist * CHUNK:(dist + 1) * CHUNK].astype(bf16)
+
+    @pl.when(i == 0)
+    def _():
+        pl.semaphore_wait(pltpu.get_barrier_semaphore(), 2 * (RING - 1))
+
+    @pl.when(i < n_col)
+    def _():
+        for side in range(2):
+            for dist in range(1, RING):
+                part_copy(side, dist, i).start()
+
+    @pl.when(i == n_col)
+    def _():
+        x_copy().wait()
+
+    @pl.when(i >= n_col)
+    def _():
+        b = i - n_col
+        cols = pl.ds(pl.multiple_of(b * width, width), width)
+        for side in range(2):
+            acc = own_s[side, b]
+            for dist in range(1, RING):
+                part_copy(side, dist, b).wait()
+                acc = acc + recv_s[side, dist - 1, b].astype(f32)
+            at = side * CHUNK
+            out_ref[at:at + CHUNK, :] = (x_s[at:at + CHUNK, cols].astype(f32) + acc).astype(bf16)
+
+
+def out_call(g_all, w_out, w_got, x_blk):
+    inner, d_model = w_out.shape
+    rows = 2 * CHUNK
+    width = min(512, d_model)
+    n_col = d_model // width
+    f32, bf16 = jnp.float32, jnp.bfloat16
+
+    def column(i):
+        return jnp.minimum(i, n_col - 1)
+
+    return pl.pallas_call(
+        functools.partial(out_kernel, n_col),
+        grid=(2 * n_col,),
+        out_shape=jax.ShapeDtypeStruct((rows, d_model), bf16),
+        in_specs=[pl.BlockSpec(g_all.shape, lambda i: (0, 0, 0, 0), pipeline_mode=pl.Buffered(1)),
+                  pl.BlockSpec((inner, width), lambda i: (0, column(i))),
+                  pl.BlockSpec((2 * (RING - 1), inner, width), lambda i: (0, 0, column(i))),
+                  pl.BlockSpec(memory_space=pl.ANY)],
+        out_specs=pl.BlockSpec((rows, width), lambda i: (0, jnp.maximum(i - n_col, 0))),
+        scratch_shapes=[
+            pltpu.VMEM((2, RING - 1, n_col, CHUNK, width), bf16),
+            pltpu.VMEM((2, RING - 1, n_col, CHUNK, width), bf16),
+            pltpu.VMEM((2, n_col, CHUNK, width), f32),
+            pltpu.VMEM((rows, d_model), bf16),
+            pltpu.SemaphoreType.DMA,
+            pltpu.SemaphoreType.DMA((2, RING - 1, n_col)),
+            pltpu.SemaphoreType.DMA((2, RING - 1, n_col)),
+        ],
+        compiler_params=pltpu.CompilerParams(collective_id=1, has_side_effects=True, vmem_limit_bytes=60 * 1024 * 1024,
+                                             dimension_semantics=('arbitrary',)),
+        cost_estimate=pl.CostEstimate(flops=2 * 2 * 4 * CHUNK * 4 * inner * d_model, bytes_accessed=40 << 20, transcendentals=0),
+    )(g_all, w_out, w_got, x_blk)
 
 
 def solution(mesh):
-    n_model = mesh.shape['tp']
     n_seq = mesh.shape['sp']
 
     def device_fn(x_blk, w_z, w_x, w_bc, w_dt, a_neg, dt_bias, d_skip, w_out):
-        tokens = x_blk.shape[0]
-        inner, d_model = w_out.shape
-        rows = tokens // n_model
-        half = d_model // 2
-        core = lax.axis_index('sp') % 2
-        pair = [(i, i ^ 1) for i in range(n_seq)]
-        w_half = lax.dynamic_slice_in_dim(w_out, core * half, half, axis=1)
-        w_all = lax.all_gather(w_half, 'tp', axis=0, tiled=True)
-        g = scan_call(x_blk, w_z, w_x, w_bc, w_dt, a_neg, dt_bias, d_skip, n_seq)
-        g_mine = lax.all_to_all(g.reshape(n_model, rows, inner), 'tp', 0, 0, tiled=True)
-        g_mine = g_mine.transpose(1, 0, 2).reshape(rows, n_model * inner)
-        g_other = lax.ppermute(g_mine, 'sp', pair)
-        out_other = jnp.dot(g_other, w_all, preferred_element_type=jnp.float32)
-        back = lax.ppermute(out_other, 'sp', pair)
-        out_mine = jnp.dot(g_mine, w_all, preferred_element_type=jnp.float32)
-        first = core == 0
-        mixed = jnp.concatenate([jnp.where(first, out_mine, back), jnp.where(first, back, out_mine)], axis=1)
-        resid = lax.dynamic_slice_in_dim(x_blk, lax.axis_index('tp') * rows, rows, axis=0)
-        return (resid.astype(jnp.float32) + mixed).astype(jnp.bfloat16)
+        g_all, w_got = scan_call(x_blk, w_z, w_x, w_bc, w_dt, a_neg, dt_bias, d_skip, w_out, n_seq)
+        return out_call(g_all, w_out, w_got, x_blk)
 
     in_specs = (P(('dp', 'sp'), None), P(None, 'tp'), P(None, 'tp'), P(None, None), P(None, 'tp'), P('tp'), P('tp'), P('tp'), P('tp', None))
     out_specs = P(('dp', 'sp', 'tp'), None)

time: 301 us -> 203 us (0.67)
  blocking collectives: 102 us -> 0 us
  Pallas kernels: 109 us -> 192 us
  matrix products: 32.6 us -> 0 us
  waiting for transfers between devices: 19.9 us -> 0 us
  between operations: 13.5 us -> 0.03 us
  local copies, waits for them, and re-layouts: 15.4 us -> 8.97 us
  other arithmetic: 5.53 us -> 0.66 us
    all_to_all x1 -> x0, blocking collectives: 102 us -> none  [device_fn(): lax.all_to_all(g.reshape(n_model, rows, inner), 'tp', 0, 0, tiled=True)]
    pallas_call x0 -> x1, Pallas kernels: none -> 65.1 us  [out_call(): pl.pallas_call(functools.partial(out_kernel, n_col), grid=(2 * n_col,), o...]
    dot_general x2 -> x0, matrix products: 32.6 us -> none  [the longest x1 16.3 us: device_fn(): out_other = jnp.dot(g_other, w_all, preferred_element_type=jnp.float32)]
    pallas_call x1, Pallas kernels: 109 us -> 127 us  [scan_call(): pl.pallas_call(functools.partial(scan_kernel, n_blk, n_seq, heads, head_d...]
    all_gather x1 -> x0, waiting for transfers between devices: 13 us -> none  [device_fn(): w_all = lax.all_gather(w_half, 'tp', axis=0, tiled=True)]
    ppermute x2 -> x0, waiting for transfers between devices: 6.92 us -> none  [the longest x1 6.92 us: device_fn(): g_other = lax.ppermute(g_mine, 'sp', pair)]
    reshape x1 -> x0, local copies, waits for them, and re-layouts: 6.44 us -> none  [device_fn(): g.reshape(n_model, rows, inner)]
    convert_element_type x1 -> x0, other arithmetic: 3.56 us -> none  [device_fn(): return (resid.astype(jnp.float32) + mixed).astype(jnp.bfloat16)]
  transfers between devices with their start and end apart: 3 -> 0, of which waited for: 2 -> 0; matrix products, arithmetic and copies ran while one was open for 9% -> 0% of each run, Pallas kernels for 36% -> 0%
where the time goes in v2:
time: 203 us; the launch traced here: 202 us
  Pallas kernels  192 us (95%)
  local copies, waits for them, and re-layouts  8.97 us (4%)
    pallas_call x1, Pallas kernels, scan_call(): pl.pallas_call(functools.partial(scan_kernel, n_blk, n_seq, heads, head_d...  127 us
    pallas_call x1, Pallas kernels, out_call(): pl.pallas_call(functools.partial(out_kernel, n_col), grid=(2 * n_col,), o...  65.1 us
    unnamed x2, local copies, waits for them, and re-layouts  4.44 us

profile of v2, /device:TPU:32, one launch (start us, length us, event | category | flops | bytes accessed | tf_op | source)
XLA Modules:
  0.0 201.5 jit_solution(5680973144507577744)
XLA Ops:
  0.0 0.7 broadcast_multiply_fusion
  0.7 0.1 broadcast_in_dim.8
  0.7 0.7 broadcast_in_dim_reshape.3.skip_ref
  1.4 1.3 broadcast_in_dim.7.aneg_ref
  2.7 1.3 broadcast_in_dim.6.bias_ref
  4.0 1.3 copy.10
  5.3 1.2 pad.4.wdt_ref
  6.5 126.7 %shard_map.91 = (bf16[2,4,512,512]{3,2,1,0:T(8,128)(2,1)}, bf16[6,512,4096]{2,1,0:T(8,128)(2,1)}) custom-call(bf16[4096,4096]{1,0:T(8,128)(2,1)} %x_ref.3, bf16[4096,512]{1,0:T(8,128)(2,1)} %wz_ref.1, bf16[4096,512]{1,0:T(8,128)(2,1)} %wx_ref.1, bf16[4096,256]{1,0:T(8,128)(2,1)} %wbc_ref.1, bf16[4096,128]{1,0:T(8,128)(2,1)} %pad.4.wdt_ref, ...), custom_call_target="tpu_custom_call" | custom-call | flops 141733920768 | bytes 62914560 | tf_op jit(solution)/shard_map/pallas_call | solution.py:298
  133.3 65.1 %shard_map.92 = bf16[256,4096]{1,0:T(8,128)(2,1)} custom-call(bf16[2,4,512,512]{3,2,1,0:T(8,128)(2,1)} %get-tuple-element.7.ga_ref, bf16[512,4096]{1,0:T(8,128)(2,1)} %wo_ref.3, bf16[6,512,4096]{2,1,0:T(8,128)(2,1)} %get-tuple-element.8.wg_ref, bf16[4096,4096]{1,0:T(8,128)(2,1)} %x_ref.3), custom_call_target="tpu_custom_call" | custom-call | flops 17179869184 | bytes 41943040 | tf_op jit(solution)/shard_map/pallas_call | solution.py:408
  198.4 3.1 %copy.12 = bf16[256,4096]{1,0:T(8,128)(2,1)} copy(bf16[256,4096]{1,0:T(8,128)(2,1)} %shard_map.92) | data formatting | bytes 4194304

commit v3 on v2

--- a/solution.py
+++ b/solution.py
@@ -50,8 +50,8 @@
     return lax.rem(z + dist, RING) * RING + y
 
 
-def scan_kernel(n_blk, n_seq, heads, head_dim, x_ref, wz_ref, wx_ref, wbc_ref, wdt_ref, bias_ref, aneg_ref, skip_ref, wo_ref, ga_ref, wg_ref,
-                z_s, u_s, bc_s, sf_s, sb_s, f_s, g_s, dt_s, ci_s, ce_s, le_s, lt_s, e_s, msg_s, rcv_s, send_sem, recv_sem, ws_sem, wr_sem, gs_sem, gr_sem, own_sem):
+def scan_kernel(n_blk, n_seq, heads, head_dim, x_ref, wz_ref, wx_ref, wbc_ref, wdt_ref, bias_sm, aneg_sm, skip_sm, wo_ref, ga_ref, wg_ref,
+                z_s, u_s, bc_s, sf_s, sb_s, f_s, g_s, dt_s, ci_s, ce_s, le_s, lt_s, e_s, msg_s, rcv_s, bias_ref, aneg_ref, skip_ref, wz_s, wz_sem, send_sem, recv_sem, ws_sem, wr_sem, gs_sem, gr_sem, own_sem):
     i = pl.program_id(0)
     me = lax.axis_index('sp')
     rows = x_ref.shape[0]
@@ -69,6 +69,10 @@
             device_id={'sp': dest}, device_id_type=pl.DeviceIdType.MESH)
 
     zy = tp_coords()
+    z_first, y_first = n_blk, 2 * n_blk
+
+    def wz_copy():
+        return pltpu.make_async_copy(wz_ref, wz_s, wz_sem)
 
     def weight_copy(k):
         part = wo_ref.shape[0] // 2
@@ -111,6 +115,17 @@
         pl.semaphore_wait(barrier, n_seq - 1 + 2 * (RING - 1))
         for k in range(4):
             weight_copy(k).start()
+        wz_copy().start()
+        head = lax.broadcasted_iota(jnp.int32, bias_ref.shape, 0)
+        owner = lax.broadcasted_iota(jnp.int32, skip_ref.shape, 1) // head_dim
+        bias, aneg, skip = jnp.zeros_like(bias_ref), jnp.zeros_like(aneg_ref), jnp.zeros_like(skip_ref)
+        for h in range(heads):
+            bias = jnp.where(head == h, bias_sm[h], bias)
+            aneg = jnp.where(head == h, aneg_sm[h], aneg)
+            skip = jnp.where(owner == h, 2.0 * skip_sm[h], skip)
+        bias_ref[...] = bias
+        aneg_ref[...] = aneg
+        skip_ref[...] = skip
         k = lax.broadcasted_iota(jnp.int32, e_s.shape, 0)
         j = lax.broadcasted_iota(jnp.int32, e_s.shape, 1)
         hit = (k // (3 * heads) == j // inner) & (k % heads == (j % inner) // head_dim)
@@ -123,14 +138,13 @@
     def _():
         base = pl.multiple_of(i * rows, rows)
         xb = x_ref[...]
-        raw = jnp.dot(xb, wdt_ref[...], preferred_element_type=f32)
+        raw = lax.dot_general(xb, wdt_ref[...], (((1,), (1,)), ((), ())), preferred_element_type=f32)
         bc_s[pl.ds(base, rows), :] = jnp.dot(xb, wbc_ref[...], preferred_element_type=f32).astype(bf16)
         u_s[pl.ds(base, rows), :] = jnp.dot(xb, wx_ref[...], preferred_element_type=f32).astype(bf16)
-        z_s[pl.ds(base, rows), :] = jnp.dot(xb, wz_ref[...], preferred_element_type=f32).astype(bf16)
         for c in range(per_blk):
             cc = i * per_blk + c
             at = pl.multiple_of(base + c * CHUNK, CHUNK)
-            dt = softplus(raw[c * CHUNK:(c + 1) * CHUNK, :].T[:heads, :] + bias_ref[...])
+            dt = softplus(raw[c * CHUNK:(c + 1) * CHUNK, :].T + bias_ref[...])
             la = dt * aneg_ref[...]
             ci = cumsum_lanes(la, lane)
             ce = ci - la
@@ -166,12 +180,24 @@
         for s in range(1, n_seq):
             peer_copy(s).start()
 
-    @pl.when(i == n_blk)
+    @pl.when(i == z_first)
+    def _():
+        wz_copy().wait()
+
+    @pl.when((i >= z_first) & (i < y_first))
+    def _():
+        base = pl.multiple_of((i - z_first) * rows, rows)
+        z_s[pl.ds(base, rows), :] = jnp.dot(x_ref[...], wz_s[...], preferred_element_type=f32).astype(bf16)
+
+    @pl.when(i == z_first + n_blk // 2)
     def _():
         for k in range(4):
             weight_copy(k).wait()
         for k in range(4, 12):
             weight_copy(k).start()
+
+    @pl.when(i == y_first)
+    def _():
         for s in range(1, n_seq):
             peer_copy(s).wait()
 
@@ -204,9 +230,9 @@
 
         lax.fori_loop(0, n_ch, back, 0)
 
-    @pl.when(i >= n_blk)
-    def _():
-        blk = i - n_blk
+    @pl.when(i >= y_first)
+    def _():
+        blk = i - y_first
         base = pl.multiple_of(blk * rows, rows)
         trow = lax.broadcasted_iota(jnp.int32, (CHUNK, CHUNK), 0)
         tcol = lax.broadcasted_iota(jnp.int32, (CHUNK, CHUNK), 1)
@@ -259,14 +285,14 @@
             def _():
                 gate_copy(side, dist, group, at).start()
 
-    @pl.when(i == n_blk + n_blk // 2)
+    @pl.when(i == y_first + n_blk // 2)
     def _():
         for k in range(4, 8):
             weight_copy(k).wait()
         for k in range(12, 14):
             weight_copy(k).start()
 
-    @pl.when(i == 2 * n_blk - 1)
+    @pl.when(i == 3 * n_blk - 1)
     def _():
         for side in range(2):
             for group in range(RING):
@@ -286,10 +312,7 @@
     rows = min(512, tokens)
     n_blk = tokens // rows
     n_ch = tokens // CHUNK
-    w_dt = jnp.pad(w_dt, ((0, 0), (0, CHUNK - heads)))
-    bias = jnp.broadcast_to(dt_bias[:, None], (heads, CHUNK))
-    aneg = jnp.broadcast_to(a_neg[:, None], (heads, CHUNK))
-    skip = jnp.repeat(2.0 * d_skip, head_dim)[None, :]
+    w_dt = w_dt.T
     f32, bf16 = jnp.float32, jnp.bfloat16
 
     def whole(a):
@@ -297,11 +320,12 @@
 
     return pl.pallas_call(
         functools.partial(scan_kernel, n_blk, n_seq, heads, head_dim),
-        grid=(2 * n_blk,),
+        grid=(3 * n_blk,),
         out_shape=(jax.ShapeDtypeStruct((2, RING, tokens // (2 * RING), inner), bf16),
                    jax.ShapeDtypeStruct((2 * (RING - 1),) + w_out.shape, bf16)),
-        in_specs=[pl.BlockSpec((rows, d_model), lambda i: (jnp.minimum(i, n_blk - 1), 0))]
-        + [whole(a) for a in (w_z, w_x, w_bc, w_dt, bias, aneg, skip)] + [pl.BlockSpec(memory_space=pl.ANY)],
+        in_specs=[pl.BlockSpec((rows, d_model), lambda i: (jnp.where(i < n_blk, i, jnp.minimum(i - n_blk, n_blk - 1)), 0)),
+                  pl.BlockSpec(memory_space=pl.ANY)]
+        + [whole(a) for a in (w_x, w_bc, w_dt)] + [pl.BlockSpec(memory_space=pltpu.SMEM)] * 3 + [pl.BlockSpec(memory_space=pl.ANY)],
         out_specs=(pl.BlockSpec(memory_space=pl.ANY), pl.BlockSpec(memory_space=pl.ANY)),
         scratch_shapes=[
             pltpu.VMEM((tokens, inner), bf16),
@@ -319,6 +343,11 @@
             pltpu.VMEM((CHUNK, 3 * inner), bf16),
             pltpu.VMEM((2, n_state + MSG_PAD, inner), bf16),
             pltpu.VMEM((n_seq - 1, n_state + MSG_PAD, inner), bf16),
+            pltpu.VMEM((heads, CHUNK), f32),
+            pltpu.VMEM((heads, CHUNK), f32),
+            pltpu.VMEM((1, inner), f32),
+            pltpu.VMEM(w_z.shape, bf16),
+            pltpu.SemaphoreType.DMA,
             pltpu.SemaphoreType.DMA((n_seq - 1,)),
             pltpu.SemaphoreType.DMA((n_seq - 1,)),
             pltpu.SemaphoreType.DMA((14,)),
@@ -330,7 +359,7 @@
         compiler_params=pltpu.CompilerParams(collective_id=0, has_side_effects=True, vmem_limit_bytes=60 * 1024 * 1024,
                                              dimension_semantics=('arbitrary',)),
         cost_estimate=pl.CostEstimate(flops=2 * tokens * d_model * (2 * inner + 3 * n_state) * 3, bytes_accessed=60 << 20, transcendentals=0),
-    )(x_blk, w_z, w_x, w_bc, w_dt, bias, aneg, skip, w_out)
+    )(x_blk, w_z, w_x, w_bc, w_dt, dt_bias, a_neg, d_skip, w_out)
 
 
 def out_kernel(n_col, ga_ref, wo_ref, wg_ref, x_ref, out_ref, send_s, recv_s, own_s, x_s, x_sem, send_sem, recv_sem):

time: 203 us -> 182 us (0.90)
  Pallas kernels: 192 us -> 178 us
  local copies, waits for them, and re-layouts: 8.97 us -> 3.13 us
    pallas_call x1, Pallas kernels: 127 us -> 115 us  [scan_call(): pl.pallas_call(functools.partial(scan_kernel, n_blk, n_seq, heads, head_d...]
    pallas_call x1, Pallas kernels: 65.1 us -> 62.4 us  [out_call(): pl.pallas_call(functools.partial(out_kernel, n_col), grid=(2 * n_col,), o...]
    broadcast_in_dim x3 -> x0, local copies, waits for them, and re-layouts: 2.69 us -> none  [the longest x1 1.31 us: scan_call(): bias = jnp.broadcast_to(dt_bias[:, None], (heads, CHUNK))]
    unnamed x2 -> x1, local copies, waits for them, and re-layouts: 4.44 us -> 3.13 us
where the time goes in v3:
time: 182 us; the launch traced here: 181 us
  Pallas kernels  178 us (98%)
  local copies, waits for them, and re-layouts  3.13 us (2%)
    pallas_call x1, Pallas kernels, scan_call(): pl.pallas_call(functools.partial(scan_kernel, n_blk, n_seq, heads, head_d...  115 us
    pallas_call x1, Pallas kernels, out_call(): pl.pallas_call(functools.partial(out_kernel, n_col), grid=(2 * n_col,), o...  62.4 us

profile of v3, /device:TPU:32, one launch (start us, length us, event | category | flops | bytes accessed | tf_op | source)
XLA Modules:
  0.0 180.7 jit_solution(5852104960400035803)
XLA Ops:
  0.0 115.2 %shard_map.91 = (bf16[2,4,512,512]{3,2,1,0:T(8,128)(2,1)}, bf16[6,512,4096]{2,1,0:T(8,128)(2,1)}) custom-call(bf16[4096,4096]{1,0:T(8,128)(2,1)} %x_ref.3, bf16[4096,512]{1,0:T(8,128)(2,1)} %wz_ref.1, bf16[4096,512]{1,0:T(8,128)(2,1)} %wx_ref.1, bf16[4096,256]{1,0:T(8,128)(2,1)} %wbc_ref.1, bf16[8,4096]{1,0:T(8,128)(2,1)} %bitcast.1, f32[8]{0:T(128)} %bias_sm.1, ...), custom_call_target="tpu_custom_call" | custom-call | flops 141733920768 | bytes 62914560 | tf_op jit(solution)/shard_map/pallas_call | solution.py:321
  115.2 62.4 %shard_map.92 = bf16[256,4096]{1,0:T(8,128)(2,1)} custom-call(bf16[2,4,512,512]{3,2,1,0:T(8,128)(2,1)} %get-tuple-element.7.ga_ref, bf16[512,4096]{1,0:T(8,128)(2,1)} %wo_ref.3, bf16[6,512,4096]{2,1,0:T(8,128)(2,1)} %get-tuple-element.8.wg_ref, bf16[4096,4096]{1,0:T(8,128)(2,1)} %x_ref.3), custom_call_target="tpu_custom_call" | custom-call | flops 17179869184 | bytes 41943040 | tf_op jit(solution)/shard_map/pallas_call | solution.py:437
  177.6 3.1 %copy.11 = bf16[256,4096]{1,0:T(8,128)(2,1)} copy(bf16[256,4096]{1,0:T(8,128)(2,1)} %shard_map.92) | data formatting | bytes 4194304

commit v4 on v3

--- a/solution.py
+++ b/solution.py
@@ -10,6 +10,7 @@
 CHUNK = 128
 MSG_PAD = 16
 RING = 4
+SHARE = 16
 
 
 def split3(v):
@@ -51,7 +52,7 @@
 
 
 def scan_kernel(n_blk, n_seq, heads, head_dim, x_ref, wz_ref, wx_ref, wbc_ref, wdt_ref, bias_sm, aneg_sm, skip_sm, wo_ref, ga_ref, wg_ref,
-                z_s, u_s, bc_s, sf_s, sb_s, f_s, g_s, dt_s, ci_s, ce_s, le_s, lt_s, e_s, msg_s, rcv_s, bias_ref, aneg_ref, skip_ref, wz_s, wz_sem, send_sem, recv_sem, ws_sem, wr_sem, gs_sem, gr_sem, own_sem):
+                z_s, u_s, bc_s, sf_s, sb_s, f_s, g_s, dt_s, ci_s, ce_s, le_s, lt_s, e_s, msg_s, rcv_s, bias_ref, aneg_ref, skip_ref, wx_s, wbc_s, wz_s, load_sem, send_sem, recv_sem, ws_sem, wr_sem, gs_sem, gr_sem, own_sem):
     i = pl.program_id(0)
     me = lax.axis_index('sp')
     rows = x_ref.shape[0]
@@ -71,28 +72,63 @@
     zy = tp_coords()
     z_first, y_first = n_blk, 2 * n_blk
 
-    def wz_copy():
-        return pltpu.make_async_copy(wz_ref, wz_s, wz_sem)
-
-    def weight_copy(k):
-        part = wo_ref.shape[0] // 2
-        mine = pl.multiple_of(lax.rem(me, 2) * part, part)
-        if k < 8:
-            axis, back = k // 2 % 2, k % 2
-            dist = RING - 1 if back else 1
-            if k < 4:
-                rows_at, src, slot = pl.ds(mine, part), wo_ref, dist
-            else:
-                rows_at = pl.ds(pl.multiple_of(mine + back * (part // 2), part // 2), part // 2)
-                src, slot = wg_ref.at[axis * 3 + dist - 1], 2
-            dest = {'tp': ring_peer(zy, axis, dist)}
-        else:
-            axis, slot = ((k - 8) // 2, (1, 3)[k % 2]) if k < 12 else (k - 12, 2)
-            rows_at, src = pl.ds(mine, part), wg_ref.at[axis * 3 + slot - 1]
-            dest = {'sp': me + 1 - 2 * lax.rem(me, 2)}
+    def load(k):
+        src, dst = ((wx_ref, wx_s), (wbc_ref, wbc_s), (wz_ref, wz_s))[k]
+        return pltpu.make_async_copy(src, dst, load_sem.at[k])
+
+    n_chip = n_seq // 2
+    chip, core = me // 2, lax.rem(me, 2)
+    half = wo_ref.shape[0] // 2
+    whole_rows = half - n_chip * SHARE
+
+    def span(shared, everyone=False):
+        at = core * half
+        if not shared:
+            return at, whole_rows
+        if everyone:
+            return at + whole_rows, n_chip * SHARE
+        return at + whole_rows + chip * SHARE, SHARE
+
+    def weight_copy(k, src, slot, at, size, dest):
+        rows_at = pl.ds(pl.multiple_of(at, 8), size)
         return pltpu.make_async_remote_copy(
-            src_ref=src.at[rows_at, :], dst_ref=wg_ref.at[axis * 3 + slot - 1, rows_at, :], send_sem=ws_sem.at[k], recv_sem=wr_sem.at[k],
+            src_ref=src.at[rows_at, :], dst_ref=wg_ref.at[slot, rows_at, :], send_sem=ws_sem.at[k], recv_sem=wr_sem.at[k],
             device_id=dest, device_id_type=pl.DeviceIdType.MESH)
+
+    def ring_copies(hop):
+        out = []
+        for axis in range(2):
+            for back in range(2):
+                dist = RING - 1 if back else 1
+                for shared in range(2):
+                    at, size = span(shared)
+                    k = ((hop * 2 + axis) * 2 + back) * 2 + shared
+                    dest = {'tp': ring_peer(zy, axis, dist)}
+                    if hop == 0:
+                        out.append(weight_copy(k, wo_ref, axis * 3 + dist - 1, at, size, dest))
+                    else:
+                        out.append(weight_copy(k, wg_ref.at[axis * 3 + dist - 1], axis * 3 + 1, at + back * (size // 2), size // 2, dest))
+        return out
+
+    near, opposite = (0, 2, 3, 5), (1, 4)
+
+    def along_x(slots):
+        at, size = span(1)
+        return [weight_copy(16 + slot * (n_chip - 1) + d - 1, wg_ref.at[slot], slot, at, size, {'sp': lax.rem(chip + d, n_chip) * 2 + core})
+                for slot in slots for d in range(1, n_chip)]
+
+    def to_partner(slots, shared):
+        at, size = span(shared, everyone=True)
+        first = 16 + 6 * (n_chip - 1)
+        return [weight_copy(first + slot * 2 + shared, wg_ref.at[slot], slot, at, size, {'sp': chip * 2 + 1 - core}) for slot in slots]
+
+    def start(copies):
+        for c in copies:
+            c.start()
+
+    def wait(copies):
+        for c in copies:
+            c.wait()
 
     def gate_copy(side, dist, group, at):
         return pltpu.make_async_remote_copy(
@@ -107,15 +143,15 @@
     @pl.when(i == 0)
     def _():
         barrier = pltpu.get_barrier_semaphore()
+        for k in range(3):
+            load(k).start()
         for s in range(1, n_seq):
             pl.semaphore_signal(barrier, inc=1, device_id={'sp': lax.rem(me + s, n_seq)}, device_id_type=pl.DeviceIdType.MESH)
         for axis in range(2):
             for dist in range(1, RING):
                 pl.semaphore_signal(barrier, inc=1, device_id={'tp': ring_peer(zy, axis, dist)}, device_id_type=pl.DeviceIdType.MESH)
         pl.semaphore_wait(barrier, n_seq - 1 + 2 * (RING - 1))
-        for k in range(4):
-            weight_copy(k).start()
-        wz_copy().start()
+        start(ring_copies(0))
         head = lax.broadcasted_iota(jnp.int32, bias_ref.shape, 0)
         owner = lax.broadcasted_iota(jnp.int32, skip_ref.shape, 1) // head_dim
         bias, aneg, skip = jnp.zeros_like(bias_ref), jnp.zeros_like(aneg_ref), jnp.zeros_like(skip_ref)
@@ -133,14 +169,16 @@
         f_s[...] = jnp.zeros_like(f_s)
         g_s[...] = jnp.zeros_like(g_s)
         lt_s[...] = jnp.zeros_like(lt_s)
+        load(0).wait()
+        load(1).wait()
 
     @pl.when(i < n_blk)
     def _():
         base = pl.multiple_of(i * rows, rows)
         xb = x_ref[...]
         raw = lax.dot_general(xb, wdt_ref[...], (((1,), (1,)), ((), ())), preferred_element_type=f32)
-        bc_s[pl.ds(base, rows), :] = jnp.dot(xb, wbc_ref[...], preferred_element_type=f32).astype(bf16)
-        u_s[pl.ds(base, rows), :] = jnp.dot(xb, wx_ref[...], preferred_element_type=f32).astype(bf16)
+        bc_s[pl.ds(base, rows), :] = jnp.dot(xb, wbc_s[...], preferred_element_type=f32).astype(bf16)
+        u_s[pl.ds(base, rows), :] = jnp.dot(xb, wx_s[...], preferred_element_type=f32).astype(bf16)
         for c in range(per_blk):
             cc = i * per_blk + c
             at = pl.multiple_of(base + c * CHUNK, CHUNK)
@@ -182,19 +220,17 @@
 
     @pl.when(i == z_first)
     def _():
-        wz_copy().wait()
+        load(2).wait()
 
     @pl.when((i >= z_first) & (i < y_first))
     def _():
         base = pl.multiple_of((i - z_first) * rows, rows)
         z_s[pl.ds(base, rows), :] = jnp.dot(x_ref[...], wz_s[...], preferred_element_type=f32).astype(bf16)
 
-    @pl.when(i == z_first + n_blk // 2)
-    def _():
-        for k in range(4):
-            weight_copy(k).wait()
-        for k in range(4, 12):
-            weight_copy(k).start()
+    @pl.when(i == z_first + n_blk // 4)
+    def _():
+        wait(ring_copies(0))
+        start(ring_copies(1) + along_x(near) + to_partner(near, 0))
 
     @pl.when(i == y_first)
     def _():
@@ -285,22 +321,26 @@
             def _():
                 gate_copy(side, dist, group, at).start()
 
-    @pl.when(i == y_first + n_blk // 2)
-    def _():
-        for k in range(4, 8):
-            weight_copy(k).wait()
-        for k in range(12, 14):
-            weight_copy(k).start()
+    @pl.when(i == y_first + n_blk // 4)
+    def _():
+        wait(ring_copies(1))
+        start(along_x(opposite) + to_partner(opposite, 0))
+
+    @pl.when(i == y_first + 3 * n_blk // 4)
+    def _():
+        wait(along_x(near))
+        start(to_partner(near, 1))
 
     @pl.when(i == 3 * n_blk - 1)
     def _():
+        wait(along_x(opposite))
+        start(to_partner(opposite, 1))
         for side in range(2):
             for group in range(RING):
                 own_copy(side, group, 0).wait()
                 for dist in range(1, RING):
                     gate_copy(side, dist, group, 0).wait()
-        for k in range(8, 14):
-            weight_copy(k).wait()
+        wait(to_partner(near + opposite, 0) + to_partner(near + opposite, 1))
 
 
 def scan_call(x_blk, w_z, w_x, w_bc, w_dt, a_neg, dt_bias, d_skip, w_out, n_seq):
@@ -312,6 +352,7 @@
     rows = min(512, tokens)
     n_blk = tokens // rows
     n_ch = tokens // CHUNK
+    n_copies = 16 + 6 * (n_seq // 2 - 1) + 12
     w_dt = w_dt.T
     f32, bf16 = jnp.float32, jnp.bfloat16
 
@@ -324,8 +365,8 @@
         out_shape=(jax.ShapeDtypeStruct((2, RING, tokens // (2 * RING), inner), bf16),
                    jax.ShapeDtypeStruct((2 * (RING - 1),) + w_out.shape, bf16)),
         in_specs=[pl.BlockSpec((rows, d_model), lambda i: (jnp.where(i < n_blk, i, jnp.minimum(i - n_blk, n_blk - 1)), 0)),
-                  pl.BlockSpec(memory_space=pl.ANY)]
-        + [whole(a) for a in (w_x, w_bc, w_dt)] + [pl.BlockSpec(memory_space=pltpu.SMEM)] * 3 + [pl.BlockSpec(memory_space=pl.ANY)],
+                  pl.BlockSpec(memory_space=pl.ANY), pl.BlockSpec(memory_space=pl.ANY), pl.BlockSpec(memory_space=pl.ANY), whole(w_dt)]
+        + [pl.BlockSpec(memory_space=pltpu.SMEM)] * 3 + [pl.BlockSpec(memory_space=pl.ANY)],
         out_specs=(pl.BlockSpec(memory_space=pl.ANY), pl.BlockSpec(memory_space=pl.ANY)),
         scratch_shapes=[
             pltpu.VMEM((tokens, inner), bf16),
@@ -346,12 +387,14 @@
             pltpu.VMEM((heads, CHUNK), f32),
             pltpu.VMEM((heads, CHUNK), f32),
             pltpu.VMEM((1, inner), f32),
+            pltpu.VMEM(w_x.shape, bf16),
+            pltpu.VMEM(w_bc.shape, bf16),
             pltpu.VMEM(w_z.shape, bf16),
-            pltpu.SemaphoreType.DMA,
+            pltpu.SemaphoreType.DMA((3,)),
             pltpu.SemaphoreType.DMA((n_seq - 1,)),
             pltpu.SemaphoreType.DMA((n_seq - 1,)),
-            pltpu.SemaphoreType.DMA((14,)),
-            pltpu.SemaphoreType.DMA((14,)),
+            pltpu.SemaphoreType.DMA((n_copies,)),
+            pltpu.SemaphoreType.DMA((n_copies,)),
             pltpu.SemaphoreType.DMA((2, RING, RING)),
             pltpu.SemaphoreType.DMA((2, RING, RING)),
             pltpu.SemaphoreType.DMA((2, RING)),

time: 182 us -> 182 us (level)
  no operation moved by 1% of the time
where the time goes in v4:
time: 182 us; the launch traced here: 181 us
  Pallas kernels  178 us (98%)
  local copies, waits for them, and re-layouts  3.13 us (2%)
    pallas_call x1, Pallas kernels, scan_call(): pl.pallas_call(functools.partial(scan_kernel, n_blk, n_seq, heads, head_d...  115 us
    pallas_call x1, Pallas kernels, out_call(): pl.pallas_call(functools.partial(out_kernel, n_col), grid=(2 * n_col,), o...  62.6 us

profile of v4, /device:TPU:32, one launch (start us, length us, event | category | flops | bytes accessed | tf_op | source)
XLA Modules:
  0.0 180.9 jit_solution(5001134613222655775)
XLA Ops:
  0.0 115.1 %shard_map.91 = (bf16[2,4,512,512]{3,2,1,0:T(8,128)(2,1)}, bf16[6,512,4096]{2,1,0:T(8,128)(2,1)}) custom-call(bf16[4096,4096]{1,0:T(8,128)(2,1)} %x_ref.3, bf16[4096,512]{1,0:T(8,128)(2,1)} %wz_ref.1, bf16[4096,512]{1,0:T(8,128)(2,1)} %wx_ref.1, bf16[4096,256]{1,0:T(8,128)(2,1)} %wbc_ref.1, bf16[8,4096]{1,0:T(8,128)(2,1)} %bitcast.1, f32[8]{0:T(128)} %bias_sm.1, ...), custom_call_target="tpu_custom_call" | custom-call | flops 141733920768 | bytes 62914560 | tf_op jit(solution)/shard_map/pallas_call | solution.py:362
  115.2 62.6 %shard_map.92 = bf16[256,4096]{1,0:T(8,128)(2,1)} custom-call(bf16[2,4,512,512]{3,2,1,0:T(8,128)(2,1)} %get-tuple-element.7.ga_ref, bf16[512,4096]{1,0:T(8,128)(2,1)} %wo_ref.3, bf16[6,512,4096]{2,1,0:T(8,128)(2,1)} %get-tuple-element.8.wg_ref, bf16[4096,4096]{1,0:T(8,128)(2,1)} %x_ref.3), custom_call_target="tpu_custom_call" | custom-call | flops 17179869184 | bytes 41943040 | tf_op jit(solution)/shard_map/pallas_call | solution.py:480
  177.8 3.1 %copy.11 = bf16[256,4096]{1,0:T(8,128)(2,1)} copy(bf16[256,4096]{1,0:T(8,128)(2,1)} %shard_map.92) | data formatting | bytes 4194304

commit v5 on v4

--- a/solution.py
+++ b/solution.py
@@ -256,19 +256,20 @@
 
         n_ch = n_blk * per_blk
 
-        def back(t, _):
-            c = n_ch - 1 - t
-            mine = sb_s[c]
-            g = g_s[...]
-            sb_s[c] = g
-            g_s[...] = g * jnp.exp(le_s[c][:1]) + mine
+        def sweep(t, _):
+            for ref, state, c in ((sf_s, f_s, t), (sb_s, g_s, n_ch - 1 - t)):
+                mine = ref[c]
+                before = state[...]
+                ref[c] = before
+                state[...] = before * jnp.exp(le_s[c][:1]) + mine
             return 0
 
-        lax.fori_loop(0, n_ch, back, 0)
+        lax.fori_loop(0, n_ch, sweep, 0)
 
     @pl.when(i >= y_first)
     def _():
-        blk = i - y_first
+        step = i - y_first
+        blk = 2 * lax.rem(zy[0] + 1 + step // 2, RING) + lax.rem(step + 1 - zy[1] // 2, 2)
         base = pl.multiple_of(blk * rows, rows)
         trow = lax.broadcasted_iota(jnp.int32, (CHUNK, CHUNK), 0)
         tcol = lax.broadcasted_iota(jnp.int32, (CHUNK, CHUNK), 1)
@@ -288,11 +289,9 @@
             b = bc_s[pl.ds(at, CHUNK), :n_state]
             cm = bc_s[pl.ds(at, CHUNK), n_state:]
             gram = lax.dot_general(cm, b, (((1,), (1,)), ((), ())), preferred_element_type=f32) * twice
-            f_in = f_s[...]
-            y = jnp.dot(cm, f_in.astype(bf16), preferred_element_type=f32) * w[:, inner:2 * inner]
+            y = jnp.dot(cm, sf_s[cc].astype(bf16), preferred_element_type=f32) * w[:, inner:2 * inner]
             y = y + jnp.dot(cm, sb_s[cc].astype(bf16), preferred_element_type=f32) * w[:, 2 * inner:]
             y = y + skip_ref[...] * u
-            f_s[...] = f_in * jnp.exp(le_s[cc][:1]) + sf_s[cc]
             outs = []
             for p in range(heads // 2):
                 mats = []
@@ -328,13 +327,11 @@
 
     @pl.when(i == y_first + 3 * n_blk // 4)
     def _():
-        wait(along_x(near))
-        start(to_partner(near, 1))
+        wait(along_x(near + opposite))
+        start(to_partner(near + opposite, 1))
 
     @pl.when(i == 3 * n_blk - 1)
     def _():
-        wait(along_x(opposite))
-        start(to_partner(opposite, 1))
         for side in range(2):
             for group in range(RING):
                 own_copy(side, group, 0).wait()

time: 182 us -> 174 us (0.956)
  Pallas kernels: 178 us -> 171 us
    pallas_call x1, Pallas kernels: 62.6 us -> 56.8 us  [out_call(): pl.pallas_call(functools.partial(out_kernel, n_col), grid=(2 * n_col,), o...]
where the time goes in v5:
time: 174 us
  Pallas kernels  171 us (98%)
  local copies, waits for them, and re-layouts  3.13 us (2%)
    pallas_call x1, Pallas kernels, scan_call(): pl.pallas_call(functools.partial(scan_kernel, n_blk, n_seq, heads, head_d...  114 us
    pallas_call x1, Pallas kernels, out_call(): pl.pallas_call(functools.partial(out_kernel, n_col), grid=(2 * n_col,), o...  56.8 us

profile of v5, /device:TPU:32, one launch (start us, length us, event | category | flops | bytes accessed | tf_op | source)
XLA Modules:
  0.0 173.8 jit_solution(406852928153579636)
XLA Ops:
  0.0 113.8 %shard_map.91 = (bf16[2,4,512,512]{3,2,1,0:T(8,128)(2,1)}, bf16[6,512,4096]{2,1,0:T(8,128)(2,1)}) custom-call(bf16[4096,4096]{1,0:T(8,128)(2,1)} %x_ref.3, bf16[4096,512]{1,0:T(8,128)(2,1)} %wz_ref.1, bf16[4096,512]{1,0:T(8,128)(2,1)} %wx_ref.1, bf16[4096,256]{1,0:T(8,128)(2,1)} %wbc_ref.1, bf16[8,4096]{1,0:T(8,128)(2,1)} %bitcast.1, f32[8]{0:T(128)} %bias_sm.1, ...), custom_call_target="tpu_custom_call" | custom-call | flops 141733920768 | bytes 62914560 | tf_op jit(solution)/shard_map/pallas_call | solution.py:359
  113.8 56.8 %shard_map.92 = bf16[256,4096]{1,0:T(8,128)(2,1)} custom-call(bf16[2,4,512,512]{3,2,1,0:T(8,128)(2,1)} %get-tuple-element.7.ga_ref, bf16[512,4096]{1,0:T(8,128)(2,1)} %wo_ref.3, bf16[6,512,4096]{2,1,0:T(8,128)(2,1)} %get-tuple-element.8.wg_ref, bf16[4096,4096]{1,0:T(8,128)(2,1)} %x_ref.3), custom_call_target="tpu_custom_call" | custom-call | flops 17179869184 | bytes 41943040 | tf_op jit(solution)/shard_map/pallas_call | solution.py:477
  170.6 3.1 %copy.11 = bf16[256,4096]{1,0:T(8,128)(2,1)} copy(bf16[256,4096]{1,0:T(8,128)(2,1)} %shard_map.92) | data formatting | bytes 4194304

commit v6 on v5

--- a/solution.py
+++ b/solution.py
@@ -11,6 +11,7 @@
 MSG_PAD = 16
 RING = 4
 SHARE = 16
+LAG = 3
 
 
 def split3(v):
@@ -402,16 +403,20 @@
     )(x_blk, w_z, w_x, w_bc, w_dt, dt_bias, a_neg, d_skip, w_out)
 
 
-def out_kernel(n_col, ga_ref, wo_ref, wg_ref, x_ref, out_ref, send_s, recv_s, own_s, x_s, x_sem, send_sem, recv_sem):
+def out_kernel(n_col, ga_ref, wo_ref, wg_ref, x_ref, out_ref, send_s, recv_s, own_s, near_s, x_s, x_sem, send_sem, recv_sem):
     i = pl.program_id(0)
     zy = tp_coords()
     width = wo_ref.shape[1]
     f32, bf16 = jnp.float32, jnp.bfloat16
-
-    def part_copy(side, dist, b):
+    relay, direct, joined = range(3)
+
+    def part_copy(kind, side, b):
+        dist = 1 + 2 * lax.rem(b, 2)
+        if kind == direct:
+            dist = RING - dist
         return pltpu.make_async_remote_copy(
-            src_ref=send_s.at[side, dist - 1, b], dst_ref=recv_s.at[side, dist - 1, b],
-            send_sem=send_sem.at[side, dist - 1, b], recv_sem=recv_sem.at[side, dist - 1, b],
+            src_ref=send_s.at[kind, side, b], dst_ref=recv_s.at[kind, side, b],
+            send_sem=send_sem.at[kind, side, b], recv_sem=recv_sem.at[kind, side, b],
             device_id={'tp': ring_peer(zy, 1 - side, dist)}, device_id_type=pl.DeviceIdType.MESH)
 
     def x_copy():
@@ -424,42 +429,54 @@
         x_copy().start()
         barrier = pltpu.get_barrier_semaphore()
         for axis in range(2):
-            for dist in range(1, RING):
+            for dist in (1, RING - 1):
                 pl.semaphore_signal(barrier, inc=1, device_id={'tp': ring_peer(zy, axis, dist)}, device_id_type=pl.DeviceIdType.MESH)
 
     @pl.when(i < n_col)
     def _():
+        right = lax.rem(i, 2) == 0
         for side in range(2):
             acc = jnp.dot(ga_ref[side, 0], wo_ref[...], preferred_element_type=f32)
             for dist in range(1, RING):
                 acc = acc + jnp.dot(ga_ref[side, dist], wg_ref[side * 3 + dist - 1], preferred_element_type=f32)
+            one, two, three = (acc[dist * CHUNK:(dist + 1) * CHUNK] for dist in range(1, RING))
             own_s[side, i] = acc[:CHUNK]
-            for dist in range(1, RING):
-                send_s[side, dist - 1, i] = acc[dist * CHUNK:(dist + 1) * CHUNK].astype(bf16)
+            send_s[relay, side, i] = two.astype(bf16)
+            send_s[direct, side, i] = jnp.where(right, three, one).astype(bf16)
+            near_s[side, i] = jnp.where(right, one, three)
 
     @pl.when(i == 0)
     def _():
-        pl.semaphore_wait(pltpu.get_barrier_semaphore(), 2 * (RING - 1))
+        pl.semaphore_wait(pltpu.get_barrier_semaphore(), 4)
 
     @pl.when(i < n_col)
     def _():
+        for kind in (relay, direct):
+            for side in range(2):
+                part_copy(kind, side, i).start()
+
+    @pl.when((i >= LAG) & (i < n_col + LAG))
+    def _():
+        b = i - LAG
         for side in range(2):
-            for dist in range(1, RING):
-                part_copy(side, dist, i).start()
-
-    @pl.when(i == n_col)
+            part_copy(relay, side, b).wait_recv()
+            send_s[joined, side, b] = (near_s[side, b] + recv_s[relay, side, b].astype(f32)).astype(bf16)
+        for side in range(2):
+            part_copy(joined, side, b).start()
+
+    @pl.when(i == n_col + LAG)
     def _():
         x_copy().wait()
 
-    @pl.when(i >= n_col)
-    def _():
-        b = i - n_col
+    @pl.when(i >= n_col + LAG)
+    def _():
+        b = i - n_col - LAG
         cols = pl.ds(pl.multiple_of(b * width, width), width)
         for side in range(2):
-            acc = own_s[side, b]
-            for dist in range(1, RING):
-                part_copy(side, dist, b).wait()
-                acc = acc + recv_s[side, dist - 1, b].astype(f32)
+            part_copy(relay, side, b).wait_send()
+            part_copy(direct, side, b).wait()
+            part_copy(joined, side, b).wait()
+            acc = own_s[side, b] + recv_s[direct, side, b].astype(f32) + recv_s[joined, side, b].astype(f32)
             at = side * CHUNK
             out_ref[at:at + CHUNK, :] = (x_s[at:at + CHUNK, cols].astype(f32) + acc).astype(bf16)
 
@@ -476,21 +493,22 @@
 
     return pl.pallas_call(
         functools.partial(out_kernel, n_col),
-        grid=(2 * n_col,),
+        grid=(2 * n_col + LAG,),
         out_shape=jax.ShapeDtypeStruct((rows, d_model), bf16),
         in_specs=[pl.BlockSpec(g_all.shape, lambda i: (0, 0, 0, 0), pipeline_mode=pl.Buffered(1)),
                   pl.BlockSpec((inner, width), lambda i: (0, column(i))),
                   pl.BlockSpec((2 * (RING - 1), inner, width), lambda i: (0, 0, column(i))),
                   pl.BlockSpec(memory_space=pl.ANY)],
-        out_specs=pl.BlockSpec((rows, width), lambda i: (0, jnp.maximum(i - n_col, 0))),
+        out_specs=pl.BlockSpec((rows, width), lambda i: (0, jnp.maximum(i - n_col - LAG, 0))),
         scratch_shapes=[
-            pltpu.VMEM((2, RING - 1, n_col, CHUNK, width), bf16),
-            pltpu.VMEM((2, RING - 1, n_col, CHUNK, width), bf16),
+            pltpu.VMEM((3, 2, n_col, CHUNK, width), bf16),
+            pltpu.VMEM((3, 2, n_col, CHUNK, width), bf16),
+            pltpu.VMEM((2, n_col, CHUNK, width), f32),
             pltpu.VMEM((2, n_col, CHUNK, width), f32),
             pltpu.VMEM((rows, d_model), bf16),
             pltpu.SemaphoreType.DMA,
-            pltpu.SemaphoreType.DMA((2, RING - 1, n_col)),
-            pltpu.SemaphoreType.DMA((2, RING - 1, n_col)),
+            pltpu.SemaphoreType.DMA((3, 2, n_col)),
+            pltpu.SemaphoreType.DMA((3, 2, n_col)),
         ],
         compiler_params=pltpu.CompilerParams(collective_id=1, has_side_effects=True, vmem_limit_bytes=60 * 1024 * 1024,
                                              dimension_semantics=('arbitrary',)),

time: 174 us -> 162 us (0.931)
  Pallas kernels: 171 us -> 159 us
    pallas_call x1, Pallas kernels: 56.8 us -> 45.3 us  [out_call(): pl.pallas_call(functools.partial(out_kernel, n_col), grid=(2 * n_col + LA...]
where the time goes in v6:
time: 162 us
  Pallas kernels  159 us (98%)
  local copies, waits for them, and re-layouts  3.13 us (2%)
    pallas_call x1, Pallas kernels, scan_call(): pl.pallas_call(functools.partial(scan_kernel, n_blk, n_seq, heads, head_d...  114 us
    pallas_call x1, Pallas kernels, out_call(): pl.pallas_call(functools.partial(out_kernel, n_col), grid=(2 * n_col + LA...  45.3 us

profile of v6, /device:TPU:32, one launch (start us, length us, event | category | flops | bytes accessed | tf_op | source)
XLA Modules:
  0.0 162.2 jit_solution(16928200380455777592)
XLA Ops:
  0.0 113.8 %shard_map.91 = (bf16[2,4,512,512]{3,2,1,0:T(8,128)(2,1)}, bf16[6,512,4096]{2,1,0:T(8,128)(2,1)}) custom-call(bf16[4096,4096]{1,0:T(8,128)(2,1)} %x_ref.3, bf16[4096,512]{1,0:T(8,128)(2,1)} %wz_ref.1, bf16[4096,512]{1,0:T(8,128)(2,1)} %wx_ref.1, bf16[4096,256]{1,0:T(8,128)(2,1)} %wbc_ref.1, bf16[8,4096]{1,0:T(8,128)(2,1)} %bitcast.1, f32[8]{0:T(128)} %bias_sm.1, ...), custom_call_target="tpu_custom_call" | custom-call | flops 141733920768 | bytes 62914560 | tf_op jit(solution)/shard_map/pallas_call | solution.py:360
  113.8 45.3 %shard_map.92 = bf16[256,4096]{1,0:T(8,128)(2,1)} custom-call(bf16[2,4,512,512]{3,2,1,0:T(8,128)(2,1)} %get-tuple-element.7.ga_ref, bf16[512,4096]{1,0:T(8,128)(2,1)} %wo_ref.3, bf16[6,512,4096]{2,1,0:T(8,128)(2,1)} %get-tuple-element.8.wg_ref, bf16[4096,4096]{1,0:T(8,128)(2,1)} %x_ref.3), custom_call_target="tpu_custom_call" | custom-call | flops 17179869184 | bytes 41943040 | tf_op jit(solution)/shard_map/pallas_call | solution.py:494
  159.1 3.1 %copy.11 = bf16[256,4096]{1,0:T(8,128)(2,1)} copy(bf16[256,4096]{1,0:T(8,128)(2,1)} %shard_map.92) | data formatting | bytes 4194304

commit v7 on v6

--- a/solution.py
+++ b/solution.py
@@ -12,6 +12,7 @@
 RING = 4
 SHARE = 16
 LAG = 3
+SPAN = 256
 
 
 def split3(v):
@@ -63,13 +64,6 @@
     f32, bf16 = jnp.float32, jnp.bfloat16
     lane = lax.broadcasted_iota(jnp.int32, (heads, CHUNK), 1)
 
-    def peer_copy(s):
-        dest = lax.rem(me + s, n_seq)
-        side = jnp.where(me + s < n_seq, 0, 1)
-        return pltpu.make_async_remote_copy(
-            src_ref=msg_s.at[side], dst_ref=rcv_s.at[s - 1], send_sem=send_sem.at[s - 1], recv_sem=recv_sem.at[s - 1],
-            device_id={'sp': dest}, device_id_type=pl.DeviceIdType.MESH)
-
     zy = tp_coords()
     z_first, y_first = n_blk, 2 * n_blk
 
@@ -81,6 +75,21 @@
     chip, core = me // 2, lax.rem(me, 2)
     half = wo_ref.shape[0] // 2
     whole_rows = half - n_chip * SHARE
+
+    def state_copy(k):
+        far = n_chip - 1
+        if k < far:
+            d = k + 1
+            src, slot = msg_s.at[jnp.where(chip + d < n_chip, 0, 1)], 2 * d
+            dest = lax.rem(chip + d, n_chip) * 2 + core
+        elif k < 2 * far:
+            d = k - far + 1
+            src, slot, dest = rcv_s.at[2 * d - 1], 2 * d + 1 - 2 * core, chip * 2 + 1 - core
+        else:
+            src, slot, dest = msg_s.at[core], jnp.where(core == 0, 1, n_seq - 1), chip * 2 + 1 - core
+        return pltpu.make_async_remote_copy(
+            src_ref=src, dst_ref=rcv_s.at[slot - 1], send_sem=send_sem.at[k], recv_sem=recv_sem.at[k],
+            device_id={'sp': dest}, device_id_type=pl.DeviceIdType.MESH)
 
     def span(shared, everyone=False):
         at = core * half
@@ -216,8 +225,7 @@
         for side, ref in ((0, f_s), (1, g_s)):
             msg_s[side, :n_state, :] = ref[...].astype(bf16)
             msg_s[side, n_state:, :] = tail
-        for s in range(1, n_seq):
-            peer_copy(s).start()
+        start([state_copy(k) for k in (*range(n_chip - 1), 2 * n_chip - 2)])
 
     @pl.when(i == z_first)
     def _():
@@ -233,10 +241,14 @@
         wait(ring_copies(0))
         start(ring_copies(1) + along_x(near) + to_partner(near, 0))
 
+    @pl.when(i == z_first + n_blk // 2 + 1)
+    def _():
+        wait([state_copy(k) for k in range(n_chip - 1)])
+        start([state_copy(k) for k in range(n_chip - 1, 2 * n_chip - 2)])
+
     @pl.when(i == y_first)
     def _():
-        for s in range(1, n_seq):
-            peer_copy(s).wait()
+        wait([state_copy(k) for k in range(n_chip - 1, 2 * n_chip - 1)])
 
         def log_of(s):
             t = rcv_s[s - 1, n_state:, :].astype(f32)
@@ -283,29 +295,32 @@
             dt, ci, ce = dt_s[cc], ci_s[cc], ce_s[cc]
             end = jnp.broadcast_to(ci[:, CHUNK - 1:], ci.shape)
             q = spread_operand([dt, jnp.exp(ci), jnp.exp(end - ce)], CHUNK)
-            w = jnp.dot(q, e_s[...], preferred_element_type=f32)
             col = jnp.concatenate([ci, ce, jnp.zeros((CHUNK - 2 * heads, CHUNK), f32)], axis=0).T
-            u = u_s[pl.ds(at, CHUNK), :].astype(f32)
-            udt = (u * w[:, :inner]).astype(bf16)
             b = bc_s[pl.ds(at, CHUNK), :n_state]
             cm = bc_s[pl.ds(at, CHUNK), n_state:]
             gram = lax.dot_general(cm, b, (((1,), (1,)), ((), ())), preferred_element_type=f32) * twice
-            y = jnp.dot(cm, sf_s[cc].astype(bf16), preferred_element_type=f32) * w[:, inner:2 * inner]
-            y = y + jnp.dot(cm, sb_s[cc].astype(bf16), preferred_element_type=f32) * w[:, 2 * inner:]
-            y = y + skip_ref[...] * u
-            outs = []
-            for p in range(heads // 2):
-                mats = []
-                for h in (2 * p, 2 * p + 1):
-                    d = jnp.where(later, col[:, h:h + 1] - ci[h:h + 1, :], ce[h:h + 1, :] - col[:, heads + h:heads + h + 1])
-                    mats.append((gram * jnp.exp(jnp.minimum(d, 0.0))).astype(bf16))
-                up = udt[:, p * CHUNK:(p + 1) * CHUNK]
-                zero = jnp.zeros_like(up)
-                rhs = jnp.concatenate([jnp.where(left, up, zero), jnp.where(left, zero, up)], axis=0)
-                outs.append(jnp.dot(jnp.concatenate(mats, axis=1), rhs, preferred_element_type=f32))
-            y = y + jnp.concatenate(outs, axis=1)
-            z = z_s[pl.ds(at, CHUNK), :].astype(f32)
-            z_s[pl.ds(at, CHUNK), :] = (y * (z / (1.0 + jnp.exp(-z)))).astype(bf16)
+            for lo in range(0, inner, SPAN):
+                here = slice(lo, lo + SPAN)
+                u = u_s[pl.ds(at, CHUNK), here].astype(f32)
+                wdt = jnp.dot(q, e_s[:, here], preferred_element_type=f32)
+                udt = (u * wdt).astype(bf16)
+                outs = []
+                for p in range(lo // CHUNK, (lo + SPAN) // CHUNK):
+                    mats = []
+                    for h in (2 * p, 2 * p + 1):
+                        d = jnp.where(later, col[:, h:h + 1] - ci[h:h + 1, :], ce[h:h + 1, :] - col[:, heads + h:heads + h + 1])
+                        mats.append((gram * jnp.exp(jnp.minimum(d, 0.0))).astype(bf16))
+                    up = udt[:, p * CHUNK - lo:(p + 1) * CHUNK - lo]
+                    zero = jnp.zeros_like(up)
+                    rhs = jnp.concatenate([jnp.where(left, up, zero), jnp.where(left, zero, up)], axis=0)
+                    outs.append(jnp.dot(jnp.concatenate(mats, axis=1), rhs, preferred_element_type=f32))
+                y = jnp.concatenate(outs, axis=1) if len(outs) > 1 else outs[0]
+                for ref, first in ((sf_s, inner), (sb_s, 2 * inner)):
+                    grown = jnp.dot(q, e_s[:, first + lo:first + lo + SPAN], preferred_element_type=f32)
+                    y = y + jnp.dot(cm, ref[cc, :, here].astype(bf16), preferred_element_type=f32) * grown
+                y = y + skip_ref[:, here] * u
+                z = z_s[pl.ds(at, CHUNK), here].astype(f32)
+                z_s[pl.ds(at, CHUNK), here] = (y * (z / (1.0 + jnp.exp(-z)))).astype(bf16)
         for c in range(per_blk):
             at = pl.multiple_of(base + c * CHUNK, CHUNK)
             side = c % 2

time: 162 us -> 162 us (level)
  no operation moved by 1% of the time
where the time goes in v7:
time: 162 us
  Pallas kernels  159 us (98%)
  local copies, waits for them, and re-layouts  3.13 us (2%)
    pallas_call x1, Pallas kernels, scan_call(): pl.pallas_call(functools.partial(scan_kernel, n_blk, n_seq, heads, head_d...  113 us
    pallas_call x1, Pallas kernels, out_call(): pl.pallas_call(functools.partial(out_kernel, n_col), grid=(2 * n_col + LA...  45.2 us

profile of v7, /device:TPU:32, one launch (start us, length us, event | category | flops | bytes accessed | tf_op | source)
XLA Modules:
  0.0 161.8 jit_solution(1900620266425907390)
XLA Ops:
  0.0 113.4 %shard_map.91 = (bf16[2,4,512,512]{3,2,1,0:T(8,128)(2,1)}, bf16[6,512,4096]{2,1,0:T(8,128)(2,1)}) custom-call(bf16[4096,4096]{1,0:T(8,128)(2,1)} %x_ref.3, bf16[4096,512]{1,0:T(8,128)(2,1)} %wz_ref.1, bf16[4096,512]{1,0:T(8,128)(2,1)} %wx_ref.1, bf16[4096,256]{1,0:T(8,128)(2,1)} %wbc_ref.1, bf16[8,4096]{1,0:T(8,128)(2,1)} %bitcast.1, f32[8]{0:T(128)} %bias_sm.1, ...), custom_call_target="tpu_custom_call" | custom-call | flops 141733920768 | bytes 62914560 | tf_op jit(solution)/shard_map/pallas_call | solution.py:375
  113.4 45.2 %shard_map.92 = bf16[256,4096]{1,0:T(8,128)(2,1)} custom-call(bf16[2,4,512,512]{3,2,1,0:T(8,128)(2,1)} %get-tuple-element.7.ga_ref, bf16[512,4096]{1,0:T(8,128)(2,1)} %wo_ref.3, bf16[6,512,4096]{2,1,0:T(8,128)(2,1)} %get-tuple-element.8.wg_ref, bf16[4096,4096]{1,0:T(8,128)(2,1)} %x_ref.3), custom_call_target="tpu_custom_call" | custom-call | flops 17179869184 | bytes 41943040 | tf_op jit(solution)/shard_map/pallas_call | solution.py:509
  158.7 3.1 %copy.11 = bf16[256,4096]{1,0:T(8,128)(2,1)} copy(bf16[256,4096]{1,0:T(8,128)(2,1)} %shard_map.92) | data formatting | bytes 4194304

commit v8 on v7

--- a/solution.py
+++ b/solution.py
@@ -186,13 +186,13 @@
     def _():
         base = pl.multiple_of(i * rows, rows)
         xb = x_ref[...]
-        raw = lax.dot_general(xb, wdt_ref[...], (((1,), (1,)), ((), ())), preferred_element_type=f32)
+        raw = lax.dot_general(wdt_ref[...], xb, (((1,), (1,)), ((), ())), preferred_element_type=f32)
         bc_s[pl.ds(base, rows), :] = jnp.dot(xb, wbc_s[...], preferred_element_type=f32).astype(bf16)
         u_s[pl.ds(base, rows), :] = jnp.dot(xb, wx_s[...], preferred_element_type=f32).astype(bf16)
         for c in range(per_blk):
             cc = i * per_blk + c
             at = pl.multiple_of(base + c * CHUNK, CHUNK)
-            dt = softplus(raw[c * CHUNK:(c + 1) * CHUNK, :].T + bias_ref[...])
+            dt = softplus(raw[:, c * CHUNK:(c + 1) * CHUNK] + bias_ref[...])
             la = dt * aneg_ref[...]
             ci = cumsum_lanes(la, lane)
             ce = ci - la

time: 162 us -> 168 us (1.037)
  Pallas kernels: 159 us -> 165 us
    pallas_call x1, Pallas kernels: 113 us -> 119 us  [scan_call(): pl.pallas_call(functools.partial(scan_kernel, n_blk, n_seq, heads, head_d...]
where the time goes in v8:
time: 168 us
  Pallas kernels  165 us (98%)
  local copies, waits for them, and re-layouts  3.13 us (2%)
    pallas_call x1, Pallas kernels, scan_call(): pl.pallas_call(functools.partial(scan_kernel, n_blk, n_seq, heads, head_d...  119 us
    pallas_call x1, Pallas kernels, out_call(): pl.pallas_call(functools.partial(out_kernel, n_col), grid=(2 * n_col + LA...  45.2 us

profile of v8, /device:TPU:32, one launch (start us, length us, event | category | flops | bytes accessed | tf_op | source)
XLA Modules:
  0.0 167.8 jit_solution(7620110509072875475)
XLA Ops:
  0.0 119.4 %shard_map.91 = (bf16[2,4,512,512]{3,2,1,0:T(8,128)(2,1)}, bf16[6,512,4096]{2,1,0:T(8,128)(2,1)}) custom-call(bf16[4096,4096]{1,0:T(8,128)(2,1)} %x_ref.3, bf16[4096,512]{1,0:T(8,128)(2,1)} %wz_ref.1, bf16[4096,512]{1,0:T(8,128)(2,1)} %wx_ref.1, bf16[4096,256]{1,0:T(8,128)(2,1)} %wbc_ref.1, bf16[8,4096]{1,0:T(8,128)(2,1)} %bitcast.1, f32[8]{0:T(128)} %bias_sm.1, ...), custom_call_target="tpu_custom_call" | custom-call | flops 141733920768 | bytes 62914560 | tf_op jit(solution)/shard_map/pallas_call | solution.py:375
  119.4 45.2 %shard_map.92 = bf16[256,4096]{1,0:T(8,128)(2,1)} custom-call(bf16[2,4,512,512]{3,2,1,0:T(8,128)(2,1)} %get-tuple-element.7.ga_ref, bf16[512,4096]{1,0:T(8,128)(2,1)} %wo_ref.3, bf16[6,512,4096]{2,1,0:T(8,128)(2,1)} %get-tuple-element.8.wg_ref, bf16[4096,4096]{1,0:T(8,128)(2,1)} %x_ref.3), custom_call_target="tpu_custom_call" | custom-call | flops 17179869184 | bytes 41943040 | tf_op jit(solution)/shard_map/pallas_call | solution.py:509
  164.7 3.1 %copy.11 = bf16[256,4096]{1,0:T(8,128)(2,1)} copy(bf16[256,4096]{1,0:T(8,128)(2,1)} %shard_map.92) | data formatting | bytes 4194304

commit v9 on v7

--- a/solution.py
+++ b/solution.py
@@ -11,7 +11,7 @@
 MSG_PAD = 16
 RING = 4
 SHARE = 16
-LAG = 3
+LAG = 5
 SPAN = 256
 
 
@@ -499,7 +499,7 @@
 def out_call(g_all, w_out, w_got, x_blk):
     inner, d_model = w_out.shape
     rows = 2 * CHUNK
-    width = min(512, d_model)
+    width = min(256, d_model)
     n_col = d_model // width
     f32, bf16 = jnp.float32, jnp.bfloat16
 

time: 162 us -> 164 us (1.012); the launches traced: 162 us -> 162 us
  no operation moved by 1% of the time
where the time goes in v9:
time: 164 us; the launch traced here: 162 us
  Pallas kernels  159 us (97%)
  local copies, waits for them, and re-layouts  3.13 us (2%)
    pallas_call x1, Pallas kernels, scan_call(): pl.pallas_call(functools.partial(scan_kernel, n_blk, n_seq, heads, head_d...  113 us
    pallas_call x1, Pallas kernels, out_call(): pl.pallas_call(functools.partial(out_kernel, n_col), grid=(2 * n_col + LA...  45.5 us

profile of v9, /device:TPU:32, one launch (start us, length us, event | category | flops | bytes accessed | tf_op | source)
XLA Modules:
  0.0 162.1 jit_solution(2449994252931602693)
XLA Ops:
  0.0 113.4 %shard_map.91 = (bf16[2,4,512,512]{3,2,1,0:T(8,128)(2,1)}, bf16[6,512,4096]{2,1,0:T(8,128)(2,1)}) custom-call(bf16[4096,4096]{1,0:T(8,128)(2,1)} %x_ref.3, bf16[4096,512]{1,0:T(8,128)(2,1)} %wz_ref.1, bf16[4096,512]{1,0:T(8,128)(2,1)} %wx_ref.1, bf16[4096,256]{1,0:T(8,128)(2,1)} %wbc_ref.1, bf16[8,4096]{1,0:T(8,128)(2,1)} %bitcast.1, f32[8]{0:T(128)} %bias_sm.1, ...), custom_call_target="tpu_custom_call" | custom-call | flops 141733920768 | bytes 62914560 | tf_op jit(solution)/shard_map/pallas_call | solution.py:375
  113.4 45.5 %shard_map.92 = bf16[256,4096]{1,0:T(8,128)(2,1)} custom-call(bf16[2,4,512,512]{3,2,1,0:T(8,128)(2,1)} %get-tuple-element.7.ga_ref, bf16[512,4096]{1,0:T(8,128)(2,1)} %wo_ref.3, bf16[6,512,4096]{2,1,0:T(8,128)(2,1)} %get-tuple-element.8.wg_ref, bf16[4096,4096]{1,0:T(8,128)(2,1)} %x_ref.3), custom_call_target="tpu_custom_call" | custom-call | flops 17179869184 | bytes 41943040 | tf_op jit(solution)/shard_map/pallas_call | solution.py:509
  158.9 3.1 %copy.11 = bf16[256,4096]{1,0:T(8,128)(2,1)} copy(bf16[256,4096]{1,0:T(8,128)(2,1)} %shard_map.92) | data formatting | bytes 4194304
